TPU v7x, 128 devices: a whole 4x4x4 slice. The times are simulated.
128 devices in a mesh: grp: 4 (over y), shard: 32 (over z, x, core).
Axes of the slice: x: 4, y: 4, z: 4, core: 2. Of those that a mesh axis runs over, the one named last changes fastest.
Arguments:
- bucket: int32 [786432], P(('grp', 'shard')), may hold values from 0 to 1048575
- label: int32 [786432], P(('grp', 'shard')), may hold values from 0 to 1
- group: int32 [786432], P(('grp', 'shard')), may hold values from 0 to 15
- group_weight: float32 [16], replicated, may hold values from 0.25 to 4
Outputs:
- tpr_curve: float32 [1048576], P('shard')
- precision_curve: float32 [1048576], P('shard')
- auroc: float32 [], replicated
- auprc: float32 [], replicated
All inputs are finite; a program needn't handle non-finite values.
Results may differ from a plain program's by a relative error of at most 0.0003.
Values sent between devices are 32-bit elements; how exact they have to be, the bound alone decides.
No kernel may reach another device: no remote copies, remote signals or barrier semaphores. Data moves between devices by JAX's collectives and lax.ppermute only.
A program may use at most 64 MiB of HBM per device.

v0:
```python
import jax
import jax.numpy as jnp
from jax import lax
from jax.sharding import PartitionSpec as P

LO = 256
BLOCK = 1024
HI = 4096


def copy_for_each(x, axis):
    count = lax.axis_size(axis)
    return lax.all_to_all(jnp.broadcast_to(x[None], (count, *x.shape)), axis, 0, 0, tiled=True)


def over_copies(x, axis):
    everything = copy_for_each(x, axis)
    return jnp.sum(everything, axis=0)


def laid_out(tiles, dim):
    dims = list(tiles.shape[1:])
    dims[dim] *= tiles.shape[0]
    return jnp.moveaxis(tiles, 0, dim).reshape(dims)


def collect(x, axis, dim):
    tiles = copy_for_each(x, axis)
    return laid_out(tiles, dim)


def in_one(arrays, axis):
    ends = [0]
    for a in arrays:
        ends.append(ends[-1] + a.size)
    so_far = over_copies(jnp.concatenate([a.ravel() for a in arrays]), axis)
    return tuple((so_far[b:e].reshape(a.shape) for a, b, e in zip(arrays, ends, ends[1:])))


def histogram(bucket, label, group, group_weight, start, count):
    choose = group[:, None] == jnp.arange(group_weight.shape[0])[None, :]
    weight = jnp.sum(jnp.where(choose, group_weight[None, :], 0.0), axis=1)
    labels = label.astype(jnp.float32)
    positive = (weight * labels).astype(jnp.bfloat16)
    negative = (weight * (1.0 - labels)).astype(jnp.bfloat16)
    rows = bucket.shape[0]
    width = BLOCK
    blocks = rows // width

    def accumulate(total, items):
        ids, plus, minus = items
        high = ids // LO
        low = ids % LO
        high_one = high[:, None] == start + jnp.arange(count)[None, :]
        zero = jnp.zeros((), jnp.bfloat16)
        left = jnp.stack(
            [jnp.where(high_one, plus[:, None], zero), jnp.where(high_one, minus[:, None], zero)],
            axis=2,
        )
        left = left.reshape(width, count * 2)
        low_one = (low[:, None] == jnp.arange(LO)[None, :]).astype(jnp.bfloat16)
        product = lax.dot_general(
            left, low_one, (((0,), (0,)), ((), ())), preferred_element_type=jnp.float32
        )
        return (total + product, None)

    initial = jnp.zeros((count * 2, LO), jnp.float32)
    items = (
        bucket.reshape(blocks, width),
        positive.reshape(blocks, width),
        negative.reshape(blocks, width),
    )
    total, _ = lax.scan(accumulate, initial, items)
    return total.reshape(count, 2, LO)


def on_device(bucket, label, group, group_weight):
    shards = lax.axis_size("shard")
    own_rows = HI // shards
    first_row = lax.axis_index("shard") * own_rows
    ids = lax.all_gather(bucket, "shard", axis=0, tiled=True)
    clicks = lax.all_gather(label, "shard", axis=0, tiled=True)
    groups = lax.all_gather(group, "shard", axis=0, tiled=True)
    owned = histogram(ids, clicks, groups, group_weight, first_row, own_rows)
    owned = over_copies(owned, "grp")
    upper = (jnp.arange(LO)[:, None] >= jnp.arange(LO)[None, :]).astype(jnp.float32)
    row_suffix = jnp.dot(owned.reshape(own_rows * 2, LO), upper, precision=lax.Precision.HIGHEST)
    row_totals = jnp.sum(owned, axis=2)
    strict = (jnp.arange(own_rows)[None, :] > jnp.arange(own_rows)[:, None]).astype(jnp.float32)
    after = jnp.dot(strict, row_totals, precision=lax.Precision.HIGHEST)
    range_total = jnp.sum(row_totals, axis=0)
    every = collect(range_total[None, :], "shard", 0)
    later = jnp.arange(shards) > lax.axis_index("shard")
    higher = jnp.sum(jnp.where(later[:, None], every, 0.0), axis=0)
    overall = jnp.sum(every, axis=0)
    cumulative = row_suffix.reshape(own_rows, 2, LO) + after[:, :, None] + higher[None, :, None]
    true_pos = cumulative[:, 0, :]
    false_pos = cumulative[:, 1, :]
    pos_hist = owned[:, 0, :]
    neg_hist = owned[:, 1, :]
    tpr_curve = (true_pos / overall[0]).reshape(own_rows * LO)
    precision = true_pos / jnp.maximum(true_pos + false_pos, 1.0)
    roc_part = jnp.sum(neg_hist * (2.0 * true_pos - pos_hist))
    prc_part = jnp.sum(pos_hist * precision)
    roc_sum, prc_sum = in_one((roc_part, prc_part), "shard")
    auroc = roc_sum / (2.0 * overall[0] * overall[1])
    auprc = prc_sum / overall[0]
    return (tpr_curve, precision.reshape(own_rows * LO), auroc, auprc)


def solution(mesh):
    placed = (P(("grp", "shard")), P(("grp", "shard")), P(("grp", "shard")), P())
    return jax.shard_map(
        on_device,
        mesh=mesh,
        in_specs=placed,
        out_specs=(P("shard"), P("shard"), P(), P()),
        check_vma=False,
    )
```

profile of v0, /device:TPU:1, one launch (start us, length us, event | category | flops | bytes accessed | tf_op | source)
XLA Modules:
  0.0 743.6 jit_solution(6775567408698807662)
XLA Ops:
  0.7 27.5 %all_gather.10 = s32[196608]{0:T(1024)S(1)} all-gather(s32[6144]{0:T(1024)} %param.8), channel_id=1, replica_groups=mesh['grp'=4,'shard'=32] {'shard'}, dimensions={0}, use_global_device_ids=true | all-gather | bytes 811008 | tf_op jit(solution)/shard_map/all_gather | solution.py:83
  28.2 24.2 %all_gather.11 = s32[196608]{0:T(1024)S(1)} all-gather(s32[6144]{0:T(1024)} %param.7), channel_id=1, replica_groups=mesh['grp'=4,'shard'=32] {'shard'}, dimensions={0}, use_global_device_ids=true | all-gather | bytes 811008 | tf_op jit(solution)/shard_map/all_gather | solution.py:82
  52.4 7.8 %select_reduce_fusion = f32[196608]{0:T(1024)S(1)} fusion(f32[16]{0:T(128)S(1)} %copy-done.1, s32[196608]{0:T(1024)S(1)} %all_gather.10), kind=kLoop, calls=%fused_computation.18 | loop fusion | flops 9240576 | bytes 1572928 | tf_op jit(solution)/shard_map/reduce_sum | solution.py:42
  61.0 22.6 %all_gather.9 = s32[196608]{0:T(1024)S(1)} all-gather(s32[6144]{0:T(1024)S(1)} %copy-done), channel_id=1, replica_groups=mesh['grp'=4,'shard'=32] {'shard'}, dimensions={0}, use_global_device_ids=true | all-gather | bytes 811008 | tf_op jit(solution)/shard_map/all_gather | solution.py:81
  83.8 606.3 %while.13 = (s32[]{:T(128)}, f32[256,256]{1,0:T(8,128)S(1)}, s32[192,1024]{1,0:T(8,128)S(1)}, s32[]{:T(128)}, bf16[192,1024]{1,0:T(8,128)(2,1)S(1)}, /*index=5*/bf16[192,1024]{1,0:T(8,128)(2,1)S(1)}, s32[]{:T(128)}, s32[]{:T(128)}) while((s32[]{:T(128)}, f32[256,256]{1,0:T(8,128)S(1)}, s32[192,1024]{1,0:T(8,128)S(1)}, s32[]{:T(128)}, ...), condition=%wide.region_2.3_spmd.clone, body=%wide.region_1.2_spmd.clone.sunk | while | flops 136072320 | bytes 3712107 | solution.py:73
  85.0 1.2 pad_maximum_fusion.3
  88.2 1.2 pad_maximum_fusion.3
  91.4 1.2 pad_maximum_fusion.3
  94.5 1.2 pad_maximum_fusion.3
  104.0 1.2 pad_maximum_fusion.3
  107.2 1.2 pad_maximum_fusion.3
  110.3 1.2 pad_maximum_fusion.3
  116.6 1.2 pad_maximum_fusion.3
  119.8 1.2 pad_maximum_fusion.3
  122.9 1.2 pad_maximum_fusion.3
  126.1 1.2 pad_maximum_fusion.3
  129.3 1.2 pad_maximum_fusion.3
  132.4 1.2 pad_maximum_fusion.3
  135.6 1.2 pad_maximum_fusion.3
  138.7 1.2 pad_maximum_fusion.3
  141.9 1.2 pad_maximum_fusion.3
  145.0 1.2 pad_maximum_fusion.3
  148.2 1.2 pad_maximum_fusion.3
  151.4 1.2 pad_maximum_fusion.3
  154.5 1.2 pad_maximum_fusion.3
  157.7 1.2 pad_maximum_fusion.3
  160.8 1.2 pad_maximum_fusion.3
  164.0 1.2 pad_maximum_fusion.3
  167.2 1.2 pad_maximum_fusion.3
  170.3 1.2 pad_maximum_fusion.3
  173.5 1.2 pad_maximum_fusion.3
  176.6 1.2 pad_maximum_fusion.3
  179.8 1.2 pad_maximum_fusion.3
  182.9 1.2 pad_maximum_fusion.3
  186.1 1.2 pad_maximum_fusion.3
  189.3 1.2 pad_maximum_fusion.3
  192.4 1.2 pad_maximum_fusion.3
  195.6 1.2 pad_maximum_fusion.3
  198.7 1.2 pad_maximum_fusion.3
  201.9 1.2 pad_maximum_fusion.3
  691.4 4.2 all-to-all-start
  695.6 14.7 %all-to-all-done = f32[4,128,2,256]{3,1,2,0:T(8,128)S(1)} async-done(((f32[4,128,2,256]{3,1,2,0:T(8,128)}), f32[4,128,2,256]{3,1,2,0:T(8,128)S(1)}, u32[]{:S(2)}, u32[]{:S(2)}) %all-to-all-start) | async-done | bytes 1048608 | tf_op jit(solution)/shard_map/all_to_all | solution.py:13
  711.2 6.2 all-to-all-start.1
  717.5 6.8 all-to-all-done.1
  725.5 1.4 pad_maximum_fusion.1
  727.4 4.2 all-to-all-start.2
  732.4 1.4 maximum_divide_fusion
  735.1 3.6 all-to-all-done.2
  (1529 shorter events, 557.3 us)
Async XLA Ops:
  0.6 51.7 %copy-start.1 = (f32[16]{0:T(128)S(1)}, f32[16]{0:T(128)}, u32[]{:S(2)}) copy-start(f32[16]{0:T(128)} %param.9) | copy-start | bytes 196
  60.3 0.7 copy-start
  691.4 18.9 %all-to-all-start = ((f32[4,128,2,256]{3,1,2,0:T(8,128)}), f32[4,128,2,256]{3,1,2,0:T(8,128)S(1)}, u32[]{:S(2)}, u32[]{:S(2)}) async-start(f32[4,128,2,256]{3,1,2,0:T(8,128)} %broadcast_in_dim.87), calls=%async_computation | async-start | bytes 2097152 | tf_op jit(solution)/shard_map/all_to_all | solution.py:13
  711.2 13.1 %all-to-all-start.1 = ((f32[32,1,2]{2,1,0:T(1,128)}), f32[32,1,2]{2,1,0:T(1,128)S(1)}, u32[]{:S(2)}, u32[]{:S(2)}) async-start(f32[32,1,2]{2,1,0:T(1,128)} %broadcast_in_dim.89), calls=%async_computation.1 | async-start | bytes 32768 | tf_op jit(solution)/shard_map/all_to_all | solution.py:13
  727.4 11.2 %all-to-all-start.2 = ((f32[32,1,2]{2,1,0:T(1,128)}), f32[32,1,2]{2,1,0:T(1,128)S(1)}, u32[]{:S(2)}, u32[]{:S(2)}) async-start(f32[32,1,2]{2,1,0:T(1,128)} %broadcast_in_dim.91), calls=%async_computation.2 | async-start | bytes 32768 | tf_op jit(solution)/shard_map/all_to_all | solution.py:13
where the time goes:
time: 744 us
  other arithmetic  464 us (62%)
  matrix products  91.9 us (12%)
  blocking collectives  74.3 us (10%)
  local copies, waits for them, and re-layouts  53.6 us (7%)
  waiting for transfers between devices  25.1 us (3%)
  starting transfers between devices  14.5 us (2%)
  loops' own time  13.7 us (2%)
    another operation x192, other arithmetic, accumulate(): jnp.stack([jnp.where(high_one, plus[:, None], zero), jnp.where(high_one,...  229 us
    select_n x192, other arithmetic, accumulate(): jnp.where(high_one, plus[:, None], zero)  220 us
    dot_general x192, matrix products, accumulate(): lax.dot_general(left, low_one, (((0,), (0,)), ((), ())), preferred_elemen...  91.5 us
    reshape x192, local copies, waits for them, and re-layouts, accumulate(): left = left.reshape(width, count * 2)  38.1 us
    all_gather x1, blocking collectives, on_device(): groups = lax.all_gather(group, 'shard', axis=0, tiled=True)  27.5 us
    all_to_all x3, waiting for transfers between devices, copy_for_each(): lax.all_to_all(jnp.broadcast_to(x[None], (count, *x.shape)), axis, 0, 0,...  25.1 us
    all_gather x1, blocking collectives, on_device(): clicks = lax.all_gather(label, 'shard', axis=0, tiled=True)  24.2 us
    all_gather x1, blocking collectives, on_device(): ids = lax.all_gather(bucket, 'shard', axis=0, tiled=True)  22.6 us
  transfers between devices with their start and end apart: 3, of which 3 were waited for; matrix products, arithmetic and copies ran while one was open for 0% of the time, Pallas kernels for 0%

commit v1 on v0

--- a/solution.py
+++ b/solution.py
@@ -1,11 +1,23 @@
 import jax
 import jax.numpy as jnp
 from jax import lax
+from jax.experimental import pallas as pl
+from jax.experimental.pallas import tpu as pltpu
 from jax.sharding import PartitionSpec as P
 
 LO = 256
 BLOCK = 1024
 HI = 4096
+
+AXES = ("grp", "shard")
+LANES = 128
+RANGES = 128
+RANGE_BITS = 13
+ROWS = 64
+CAP = 126
+NT = (((1,), (1,)), ((), ()))
+NN = (((1,), (0,)), ((), ()))
+HIGHEST = lax.Precision.HIGHEST
 
 
 def copy_for_each(x, axis):
@@ -74,7 +86,7 @@
     return total.reshape(count, 2, LO)
 
 
-def on_device(bucket, label, group, group_weight):
+def general(bucket, label, group, group_weight):
     shards = lax.axis_size("shard")
     own_rows = HI // shards
     first_row = lax.axis_index("shard") * own_rows
@@ -84,10 +96,10 @@
     owned = histogram(ids, clicks, groups, group_weight, first_row, own_rows)
     owned = over_copies(owned, "grp")
     upper = (jnp.arange(LO)[:, None] >= jnp.arange(LO)[None, :]).astype(jnp.float32)
-    row_suffix = jnp.dot(owned.reshape(own_rows * 2, LO), upper, precision=lax.Precision.HIGHEST)
+    row_suffix = jnp.dot(owned.reshape(own_rows * 2, LO), upper, precision=HIGHEST)
     row_totals = jnp.sum(owned, axis=2)
     strict = (jnp.arange(own_rows)[None, :] > jnp.arange(own_rows)[:, None]).astype(jnp.float32)
-    after = jnp.dot(strict, row_totals, precision=lax.Precision.HIGHEST)
+    after = jnp.dot(strict, row_totals, precision=HIGHEST)
     range_total = jnp.sum(row_totals, axis=0)
     every = collect(range_total[None, :], "shard", 0)
     later = jnp.arange(shards) > lax.axis_index("shard")
@@ -108,8 +120,226 @@
     return (tpr_curve, precision.reshape(own_rows * LO), auroc, auprc)
 
 
+def iota(shape, dim):
+    return lax.broadcasted_iota(jnp.int32, shape, dim)
+
+
+def bf16_rows(row):
+    return jnp.broadcast_to(row, (16, row.shape[1])).astype(jnp.bfloat16)
+
+
+def route_kernel(weights_ref, bucket_ref, label_ref, group_ref, out_ref,
+                 peer_s, high_s, low_s, pos_s, neg_s, one_s, left_s, right_s, acc_s):
+    blocks = bucket_ref.shape[0]
+    step = 8
+    bucket = bucket_ref[...]
+    group = group_ref[...]
+    weight = jnp.zeros(group.shape, jnp.float32)
+    for k in range(weights_ref.shape[0]):
+        weight = jnp.where(group == k, weights_ref[k], weight)
+    labels = label_ref[...].astype(jnp.float32)
+    pos_s[...] = weight * labels
+    neg_s[...] = weight * (1.0 - labels)
+    which = bucket >> RANGE_BITS
+    peer = ((which & 3) << 5) | (which >> 2)
+    peer_s[...] = peer.astype(jnp.float32)
+    high_s[...] = ((bucket >> 7) & (ROWS - 1)).astype(jnp.float32)
+    low_s[...] = (bucket & (LANES - 1)).astype(jnp.float32)
+
+    before = (iota((LANES, 2 * LANES), 0) < iota((LANES, 2 * LANES), 1)).astype(jnp.bfloat16)
+    sub = iota((16, LANES), 0)
+    unit = jnp.ones((16, LANES), jnp.bfloat16)
+    none = jnp.zeros((16, LANES), jnp.bfloat16)
+    kind = sub & 3
+    sub_f = sub.astype(jnp.float32).astype(jnp.bfloat16)
+    quarter_f = (sub >> 2).astype(jnp.float32).astype(jnp.bfloat16)
+    acc_s[...] = jnp.zeros(acc_s.shape, jnp.float32)
+
+    def chunk(i, count):
+        for u in range(step):
+            row = bf16_rows(peer_s[pl.ds(i * step + u, 1), :])
+            for k in range(8):
+                one_s[pl.ds(u * LANES + 16 * k, 16), :] = jnp.where(
+                    sub_f + jnp.bfloat16(16 * k) == row, unit, none)
+        ones = one_s[...]
+        seen = lax.dot_general(ones, before, NN, preferred_element_type=jnp.float32)
+        for u in range(step):
+            mine = ones[u * LANES:(u + 1) * LANES].astype(jnp.float32)
+            part = seen[u * LANES:(u + 1) * LANES]
+            rank = jnp.sum(mine * (part[:, :LANES] + count), axis=0, keepdims=True)
+            count = count + part[:, LANES:]
+            j = i * step + u
+            lanes = pl.ds(u * LANES, LANES)
+            rank_row = bf16_rows(jnp.minimum(rank, 255.0))
+            for k in range(8):
+                right_s[pl.ds(16 * k, 16), lanes] = jnp.where(
+                    sub_f + jnp.bfloat16(16 * k) == rank_row, unit, none)
+            high = jnp.broadcast_to(high_s[pl.ds(j, 1), :], (16, LANES))
+            low = jnp.broadcast_to(low_s[pl.ds(j, 1), :], (16, LANES))
+            pos = jnp.broadcast_to(pos_s[pl.ds(j, 1), :], (16, LANES))
+            neg = jnp.broadcast_to(neg_s[pl.ds(j, 1), :], (16, LANES))
+            value = jnp.where(kind == 0, high, jnp.where(kind == 1, low, jnp.where(kind == 2, pos, neg)))
+            value = value.astype(jnp.bfloat16)
+            row = bf16_rows(peer_s[pl.ds(j, 1), :])
+            for k in range(32):
+                left_s[pl.ds(16 * k, 16), lanes] = jnp.where(
+                    quarter_f + jnp.bfloat16(4 * k) == row, value, none)
+        acc_s[...] += lax.dot_general(left_s[...], right_s[...], NT, preferred_element_type=jnp.float32)
+        return count
+
+    count = lax.fori_loop(0, blocks // step, chunk, jnp.zeros((RANGES, LANES), jnp.float32))
+    full = jnp.max(jnp.where(count > CAP, 1.0, 0.0), axis=0, keepdims=True)
+    full = jnp.max(full, axis=1, keepdims=True)
+
+    lane = iota((RANGES, LANES), 1)
+    real = lane < CAP
+    high = acc_s[pl.ds(0, RANGES, stride=4), :]
+    low = acc_s[pl.ds(1, RANGES, stride=4), :]
+    pos = jnp.where(real, acc_s[pl.ds(2, RANGES, stride=4), :], 0.0)
+    neg = jnp.where(real, acc_s[pl.ds(3, RANGES, stride=4), :], 0.0)
+    p0 = iota((RANGES, RANGES), 0)
+    p1 = iota((RANGES, RANGES), 1)
+    r0 = ((p0 & 31) << 2) | (p0 >> 5)
+    r1 = ((p1 & 31) << 2) | (p1 >> 5)
+    above = (r1 > r0).astype(jnp.bfloat16)
+    both = jnp.concatenate([pos, neg], axis=1).astype(jnp.bfloat16)
+    later = lax.dot_general(above, both, NN, preferred_element_type=jnp.float32)
+    higher_pos = jnp.sum(later[:, :LANES], axis=1, keepdims=True)
+    higher_neg = jnp.sum(later[:, LANES:], axis=1, keepdims=True)
+    total_pos = jnp.sum(jnp.sum(pos, axis=0, keepdims=True), axis=1, keepdims=True)
+    total_neg = jnp.sum(jnp.sum(neg, axis=0, keepdims=True), axis=1, keepdims=True)
+    out_ref[pl.ds(0, RANGES, stride=4), :] = jnp.where(real, high, full)
+    out_ref[pl.ds(1, RANGES, stride=4), :] = low
+    out_ref[pl.ds(2, RANGES, stride=4), :] = jnp.where(real, pos, jnp.where(lane == CAP, higher_pos, total_pos))
+    out_ref[pl.ds(3, RANGES, stride=4), :] = jnp.where(real, neg, jnp.where(lane == CAP, higher_neg, total_neg))
+
+
+def curve_kernel(in_ref, curve_ref, part_ref, left_s, right_s):
+    step = 8
+    sub_f = iota((16, LANES), 0).astype(jnp.float32).astype(jnp.bfloat16)
+    none = jnp.zeros((16, LANES), jnp.bfloat16)
+    unit = jnp.ones((16, LANES), jnp.bfloat16)
+    real = iota((1, LANES), 1) < CAP
+
+    def chunk(i, carry):
+        hist, sums = carry
+        for u in range(step):
+            at = (i * step + u) * 4
+            lanes = pl.ds(u * LANES, LANES)
+            high = bf16_rows(in_ref[pl.ds(at, 1), :])
+            low = bf16_rows(in_ref[pl.ds(at + 1, 1), :])
+            pos = bf16_rows(jnp.where(real, in_ref[pl.ds(at + 2, 1), :], 0.0))
+            neg = bf16_rows(jnp.where(real, in_ref[pl.ds(at + 3, 1), :], 0.0))
+            for k in range(4):
+                same = sub_f + jnp.bfloat16(16 * k) == high
+                left_s[pl.ds(16 * k, 16), lanes] = jnp.where(same, pos, none)
+                left_s[pl.ds(ROWS + 16 * k, 16), lanes] = jnp.where(same, neg, none)
+            for k in range(8):
+                right_s[pl.ds(16 * k, 16), lanes] = jnp.where(
+                    sub_f + jnp.bfloat16(16 * k) == low, unit, none)
+        hist = hist + lax.dot_general(left_s[...], right_s[...], NT, preferred_element_type=jnp.float32)
+        for u in range(step // 2):
+            sums = sums + in_ref[pl.ds((i * step + 2 * u) * 4, 8), :]
+        return hist, sums
+
+    start = (jnp.zeros((2 * ROWS, LANES), jnp.float32), jnp.zeros((8, LANES), jnp.float32))
+    hist, sums = lax.fori_loop(0, RANGES // step, chunk, start)
+    sums = sums[0:4] + sums[4:8]
+    flag = sums[0:1, CAP:CAP + 1]
+    higher_pos = sums[2:3, CAP:CAP + 1]
+    total_pos = sums[2:3, CAP + 1:CAP + 2]
+    higher_neg = sums[3:4, CAP:CAP + 1]
+    total_neg = sums[3:4, CAP + 1:CAP + 2]
+    upper = (iota((LANES, LANES), 0) >= iota((LANES, LANES), 1)).astype(jnp.float32)
+    row = iota((2 * ROWS, 2 * ROWS), 0)
+    col = iota((2 * ROWS, 2 * ROWS), 1)
+    below = ((col > row) & ((col >= ROWS) == (row >= ROWS))).astype(jnp.float32)
+    in_row = lax.dot_general(hist, upper, NN, precision=HIGHEST, preferred_element_type=jnp.float32)
+    rows_after = lax.dot_general(below, hist, NN, precision=HIGHEST, preferred_element_type=jnp.float32)
+    cumulative = in_row + jnp.sum(rows_after, axis=1, keepdims=True)
+    true_pos = cumulative[:ROWS] + higher_pos
+    false_pos = cumulative[ROWS:] + higher_neg
+    pos_hist = hist[:ROWS]
+    neg_hist = hist[ROWS:]
+    precision = true_pos / jnp.maximum(true_pos + false_pos, 1.0)
+    curve_ref[0] = true_pos / total_pos
+    curve_ref[1] = precision
+    roc = jnp.sum(neg_hist * (2.0 * true_pos - pos_hist), axis=0, keepdims=True)
+    prc = jnp.sum(pos_hist * precision, axis=0, keepdims=True)
+    roc = jnp.sum(roc, axis=1, keepdims=True) / (2.0 * total_pos * total_neg)
+    prc = jnp.sum(prc, axis=1, keepdims=True) / total_pos
+    lane = iota((RANGES, 1, LANES), 2)
+    part_ref[...] = jnp.where(lane == 0, roc[None], jnp.where(lane == 1, prc[None], flag[None]))
+
+
+def join_kernel(own_ref, one_ref, two_ref, three_ref, part_ref, tpr_ref, precision_ref, roc_ref, prc_ref, flag_ref):
+    me = lax.axis_index("grp")
+    for k, ref in enumerate((own_ref, one_ref, two_ref, three_ref)):
+        source = (me - k) & 3
+        tpr_ref[source] = ref[0]
+        precision_ref[source] = ref[1]
+    sums = jnp.sum(part_ref[...].reshape(RANGES, LANES), axis=0, keepdims=True)
+    lane = iota((1, LANES), 1)
+    roc_ref[0] = jnp.sum(jnp.where(lane == 0, sums, 0.0))
+    prc_ref[0] = jnp.sum(jnp.where(lane == 1, sums, 0.0))
+    flag_ref[0] = jnp.sum(jnp.where(lane == 2, sums, 0.0))
+
+
+def vmem():
+    return pl.BlockSpec(memory_space=pltpu.VMEM)
+
+
+def smem():
+    return pl.BlockSpec(memory_space=pltpu.SMEM)
+
+
+def f32(*shape):
+    return jax.ShapeDtypeStruct(shape, jnp.float32)
+
+
+def on_device(bucket, label, group, group_weight):
+    blocks = bucket.shape[0] // LANES
+    message = pl.pallas_call(
+        route_kernel,
+        out_shape=f32(4 * RANGES, LANES),
+        in_specs=[smem(), vmem(), vmem(), vmem()],
+        out_specs=vmem(),
+        scratch_shapes=[pltpu.VMEM((blocks, LANES), jnp.float32)] * 5
+        + [pltpu.VMEM((8 * LANES, LANES), jnp.bfloat16),
+           pltpu.VMEM((4 * RANGES, 8 * LANES), jnp.bfloat16),
+           pltpu.VMEM((LANES, 8 * LANES), jnp.bfloat16),
+           pltpu.VMEM((4 * RANGES, LANES), jnp.float32)],
+        name="route",
+    )(group_weight, bucket.reshape(blocks, LANES), label.reshape(blocks, LANES), group.reshape(blocks, LANES))
+    received = lax.all_to_all(message.reshape(RANGES, 4, LANES), AXES, 0, 0, tiled=True)
+    curves, parts = pl.pallas_call(
+        curve_kernel,
+        out_shape=(f32(2, ROWS, LANES), f32(RANGES, 1, LANES)),
+        in_specs=[vmem()],
+        out_specs=(vmem(), vmem()),
+        scratch_shapes=[pltpu.VMEM((2 * ROWS, 8 * LANES), jnp.bfloat16), pltpu.VMEM((LANES, 8 * LANES), jnp.bfloat16)],
+        name="curve",
+    )(received.reshape(4 * RANGES, LANES))
+    others = [lax.ppermute(curves, "grp", [(i, (i + k) % 4) for i in range(4)]) for k in (1, 2, 3)]
+    parts = lax.all_to_all(parts, AXES, 0, 0, tiled=True)
+    tpr, precision, roc, prc, flag = pl.pallas_call(
+        join_kernel,
+        out_shape=(f32(4, ROWS, LANES), f32(4, ROWS, LANES), f32(1), f32(1), f32(1)),
+        in_specs=[vmem()] * 5,
+        out_specs=(vmem(), vmem(), smem(), smem(), smem()),
+        name="join",
+    )(curves, *others, parts)
+    quick = (tpr.reshape(4 * ROWS * LANES), precision.reshape(4 * ROWS * LANES), roc.reshape(()), prc.reshape(()))
+
+    def again(state):
+        return (jnp.zeros((), jnp.float32), *general(bucket, label, group, group_weight))
+
+    state = lax.while_loop(lambda s: s[0] > 0.0, again, (flag.reshape(()), *quick))
+    return state[1:]
+
+
 def solution(mesh):
-    placed = (P(("grp", "shard")), P(("grp", "shard")), P(("grp", "shard")), P())
+    placed = (P(AXES), P(AXES), P(AXES), P())
     return jax.shard_map(
         on_device,
         mesh=mesh,

time: 744 us -> 60.3 us (0.08)
  other arithmetic: 464 us -> 0 us
  matrix products: 91.9 us -> 0 us
  local copies, waits for them, and re-layouts: 53.6 us -> 1.25 us
  blocking collectives: 74.3 us -> 38.6 us
  waiting for transfers between devices: 25.1 us -> 0.01 us
  Pallas kernels: 0 us -> 15 us
  loops' own time: 13.7 us -> 0.92 us
  starting transfers between devices: 14.5 us -> 3.3 us
    another operation x192 -> x0, other arithmetic: 229 us -> none  [accumulate(): jnp.stack([jnp.where(high_one, plus[:, None], zero), jnp.where(high_one,...]
    select_n x384 -> x0, other arithmetic: 222 us -> none  [the longest x192 220 us: accumulate(): jnp.where(high_one, plus[:, None], zero)]
    dot_general x194 -> x0, matrix products: 91.9 us -> none  [the longest x192 91.5 us: accumulate(): lax.dot_general(left, low_one, (((0,), (0,)), ((), ())), preferred_elemen...]
    all_gather x3 -> x0, blocking collectives: 74.3 us -> none  [the longest x1 27.5 us: on_device(): groups = lax.all_gather(group, 'shard', axis=0, tiled=True)]
    all_to_all x0 -> x2, blocking collectives: none -> 38.6 us  [the longest x1 22.5 us: on_device(): lax.all_to_all(message.reshape(RANGES, 4, LANES), AXES, 0, 0, tiled=True)]
    reshape x195 -> x0, local copies, waits for them, and re-layouts: 38.6 us -> none  [the longest x192 38.1 us: accumulate(): left = left.reshape(width, count * 2)]
    all_to_all x3 -> x0, waiting for transfers between devices: 25.1 us -> none  [copy_for_each(): lax.all_to_all(jnp.broadcast_to(x[None], (count, *x.shape)), axis, 0, 0,...]
    pallas_call x0 -> x3, Pallas kernels: none -> 15 us  [the longest x1 6.7 us: on_device(): pl.pallas_call(curve_kernel, out_shape=(f32(2, ROWS, LANES), f32(RANGES,...]
  transfers between devices with their start and end apart: 3 -> 3, of which waited for: 3 -> 0; matrix products, arithmetic and copies ran while one was open for 0% -> 0% of each run, Pallas kernels for 0% -> 0%
where the time goes in v1:
time: 60.3 us; the launch traced here: 60 us
  blocking collectives  38.6 us (64%)
  Pallas kernels  15 us (25%)
  starting transfers between devices  3.3 us (5%)
  local copies, waits for them, and re-layouts  1.25 us (2%)
  loops' own time  0.92 us (2%)
  between operations  0.91 us (2%)
    all_to_all x1, blocking collectives, on_device(): lax.all_to_all(message.reshape(RANGES, 4, LANES), AXES, 0, 0, tiled=True)  22.5 us
    all_to_all x1, blocking collectives, on_device(): parts = lax.all_to_all(parts, AXES, 0, 0, tiled=True)  16.1 us
    pallas_call x1, Pallas kernels, on_device(): pl.pallas_call(curve_kernel, out_shape=(f32(2, ROWS, LANES), f32(RANGES,...  6.7 us
    pallas_call x1, Pallas kernels, on_device(): pl.pallas_call(route_kernel, out_shape=f32(4 * RANGES, LANES), in_specs=[...  6.63 us
    ppermute x3, starting transfers between devices, on_device(): lax.ppermute(curves, 'grp', [(i, (i + k) % 4) for i in range(4)])  3.3 us
    pallas_call x1, Pallas kernels, on_device(): pl.pallas_call(join_kernel, out_shape=(f32(4, ROWS, LANES), f32(4, ROWS,...  1.72 us
    unnamed x14, local copies, waits for them, and re-layouts  1.25 us
  transfers between devices with their start and end apart: 3, of which 0 were waited for; matrix products, arithmetic and copies ran while one was open for 0% of the time, Pallas kernels for 0%

profile of v1, /device:TPU:1, one launch (start us, length us, event | category | flops | bytes accessed | tf_op | source)
XLA Modules:
  0.0 60.0 jit_solution(18033019849648660138)
XLA Ops:
  0.6 0.0 copy-start
  0.6 0.0 copy-start.1
  0.7 0.0 copy-start.2
  0.7 0.0 copy-start.6
  0.7 6.6 %route.1 = f32[512,128]{1,0:T(8,128)} custom-call(f32[16]{0:T(128)} %weights_ref.1, s32[48,128]{1,0:T(8,128)} %bitcast.77, s32[48,128]{1,0:T(8,128)} %bitcast.78, s32[48,128]{1,0:T(8,128)} %bitcast.79), custom_call_target="tpu_custom_call" | custom-call | tf_op jit(solution)/shard_map/route/pallas_call | solution.py:302
  7.3 22.5 %all_to_all.23 = f32[128,4,128]{2,1,0:T(4,128)} all-to-all(f32[128,4,128]{2,1,0:T(4,128)} %bitcast.76), channel_id=1, replica_groups=mesh['grp'=4,'shard'=32] {'grp','shard'}, dimensions={0} | all-to-all | bytes 524288 | tf_op jit(solution)/shard_map/all_to_all | solution.py:314
  29.8 6.7 %curve.1 = (f32[2,64,128]{2,1,0:T(8,128)}, f32[128,1,128]{2,1,0:T(1,128)}) custom-call(f32[512,128]{1,0:T(8,128)} %bitcast.75), custom_call_target="tpu_custom_call" | custom-call | tf_op jit(solution)/shard_map/curve/pallas_call | solution.py:315
  36.5 0.3 collective-permute-start
  36.8 1.7 %collective-permute-start.1 = (f32[2,64,128]{2,1,0:T(8,128)}, f32[2,64,128]{2,1,0:T(8,128)S(1)}, u32[]{:S(2)}, u32[]{:S(2)}) collective-permute-start(f32[2,64,128]{2,1,0:T(8,128)} %get-tuple-element.136.own_ref), channel_id=1, source_target_pairs={{0,64},{32,96},{64,0},{96,32},{1,65},{33,97},{65,1},{97,33},{2,66}... | collective-permute-start | bytes 196616 | tf_op jit(solution)/shard_map/ppermute | solution.py:323
  38.4 1.4 %collective-permute-start.2 = (f32[2,64,128]{2,1,0:T(8,128)}, f32[2,64,128]{2,1,0:T(8,128)S(1)}, u32[]{:S(2)}, u32[]{:S(2)}) collective-permute-start(f32[2,64,128]{2,1,0:T(8,128)} %get-tuple-element.136.own_ref), channel_id=1, source_target_pairs={{0,96},{32,0},{64,32},{96,64},{1,97},{33,1},{65,33},{97,65},{2,98}... | collective-permute-start | bytes 196616 | tf_op jit(solution)/shard_map/ppermute | solution.py:323
  39.8 16.1 %all_to_all.24.part_ref = f32[128,1,128]{2,1,0:T(1,128)} all-to-all(f32[128,1,128]{2,1,0:T(1,128)} %get-tuple-element.137), channel_id=1, replica_groups=mesh['grp'=4,'shard'=32] {'grp','shard'}, dimensions={0} | all-to-all | bytes 131072 | tf_op jit(solution)/shard_map/all_to_all | solution.py:324
  55.9 0.0 collective-permute-done.one_ref
  55.9 0.0 copy-start.3
  55.9 0.0 collective-permute-done.1.two_ref
  55.9 0.0 copy-start.4
  55.9 0.0 collective-permute-done.2.three_ref
  55.9 0.6 copy-done.3
  56.5 0.0 copy-done.4
  56.5 0.0 copy-start.5
  56.5 0.6 %copy-done.5 = f32[2,64,128]{2,1,0:T(8,128)} copy-done((f32[2,64,128]{2,1,0:T(8,128)}, f32[2,64,128]{2,1,0:T(8,128)S(1)}, u32[]{:S(2)}) %copy-start.5) | copy-done | bytes 65560
  57.1 1.7 %join.1 = (f32[4,64,128]{2,1,0:T(8,128)}, f32[4,64,128]{2,1,0:T(8,128)}, f32[1]{0:T(128)}, f32[1]{0:T(128)}, f32[1]{0:T(128)}) custom-call(f32[2,64,128]{2,1,0:T(8,128)} %get-tuple-element.136.own_ref, f32[2,64,128]{2,1,0:T(8,128)} %copy-done.3, f32[2,64,128]{2,1,0:T(8,128)} %copy-done.4, f32[2,64,128]{2,1,0:T(8,128)} %copy-done.5, ...), custom_call_target="tpu_custom_call" | custom-call | tf_op jit(solution)/shard_map/join/pallas_call | solution.py:325
  58.9 0.0 copy-done
  58.9 0.0 copy-done.1
  58.9 0.0 copy-done.2
  58.9 0.0 copy-done.6
  58.9 0.9 %while.26 = (f32[]{:T(128)}, f32[32768]{0:T(1024)}, f32[32768]{0:T(1024)}, f32[]{:T(128)}, f32[]{:T(128)}, /*index=5*/s32[6144]{0:T(1024)S(1)}, s32[6144]{0:T(1024)S(1)}, f32[16]{0:T(128)S(1)}, s32[6144]{0:T(1024)S(1)}) while((f32[]{:T(128)}, f32[32768]{0:T(1024)}, f32[32768]{0:T(1024)}, f32[]{:T(128)}, f32[]{:T(128)}, /*index=5*/s32[6144]{0:T(1024)S(1)}, ...), condition=%region_12.13_spmd, body=%region_0.12_spmd | while | flops 349572256 | bytes 22732732 | solution.py:337
Async XLA Ops:
  0.6 58.2 %copy-start = (s32[6144]{0:T(1024)S(1)}, s32[6144]{0:T(1024)}, u32[]{:S(2)}) copy-start(s32[6144]{0:T(1024)} %param.8) | copy-start | bytes 73732
  0.6 58.2 %copy-start.1 = (s32[6144]{0:T(1024)S(1)}, s32[6144]{0:T(1024)}, u32[]{:S(2)}) copy-start(s32[6144]{0:T(1024)} %param.9) | copy-start | bytes 73732
  0.7 58.2 %copy-start.2 = (s32[6144]{0:T(1024)S(1)}, s32[6144]{0:T(1024)}, u32[]{:S(2)}) copy-start(s32[6144]{0:T(1024)} %param.10) | copy-start | bytes 73732
  0.7 58.2 %copy-start.6 = (f32[16]{0:T(128)S(1)}, f32[16]{0:T(128)}, u32[]{:S(2)}) copy-start(f32[16]{0:T(128)} %weights_ref.1) | copy-start | bytes 196
  36.5 19.4 %collective-permute-start = (f32[2,64,128]{2,1,0:T(8,128)}, f32[2,64,128]{2,1,0:T(8,128)S(1)}, u32[]{:S(2)}, u32[]{:S(2)}) collective-permute-start(f32[2,64,128]{2,1,0:T(8,128)} %get-tuple-element.136.own_ref), channel_id=1, source_target_pairs={{0,32},{32,64},{64,96},{96,0},{1,33},{33,65},{65,97},{97,1},{2,34}... | collective-permute-start | bytes 196616 | tf_op jit(solution)/shard_map/ppermute | solution.py:323
  36.8 19.1 %collective-permute-start.1 = (f32[2,64,128]{2,1,0:T(8,128)}, f32[2,64,128]{2,1,0:T(8,128)S(1)}, u32[]{:S(2)}, u32[]{:S(2)}) collective-permute-start(f32[2,64,128]{2,1,0:T(8,128)} %get-tuple-element.136.own_ref), channel_id=1, source_target_pairs={{0,64},{32,96},{64,0},{96,32},{1,65},{33,97},{65,1},{97,33},{2,66}... | collective-permute-start | bytes 196616 | tf_op jit(solution)/shard_map/ppermute | solution.py:323
  38.4 17.5 %collective-permute-start.2 = (f32[2,64,128]{2,1,0:T(8,128)}, f32[2,64,128]{2,1,0:T(8,128)S(1)}, u32[]{:S(2)}, u32[]{:S(2)}) collective-permute-start(f32[2,64,128]{2,1,0:T(8,128)} %get-tuple-element.136.own_ref), channel_id=1, source_target_pairs={{0,96},{32,0},{64,32},{96,64},{1,97},{33,1},{65,33},{97,65},{2,98}... | collective-permute-start | bytes 196616 | tf_op jit(solution)/shard_map/ppermute | solution.py:323
  55.9 0.6 %copy-start.3 = (f32[2,64,128]{2,1,0:T(8,128)}, f32[2,64,128]{2,1,0:T(8,128)S(1)}, u32[]{:S(2)}) copy-start(f32[2,64,128]{2,1,0:T(8,128)S(1)} %collective-permute-done.one_ref) | copy-start | bytes 196612
  55.9 0.6 %copy-start.4 = (f32[2,64,128]{2,1,0:T(8,128)}, f32[2,64,128]{2,1,0:T(8,128)S(1)}, u32[]{:S(2)}) copy-start(f32[2,64,128]{2,1,0:T(8,128)S(1)} %collective-permute-done.1.two_ref) | copy-start | bytes 196612
  56.5 0.6 %copy-start.5 = (f32[2,64,128]{2,1,0:T(8,128)}, f32[2,64,128]{2,1,0:T(8,128)S(1)}, u32[]{:S(2)}) copy-start(f32[2,64,128]{2,1,0:T(8,128)S(1)} %collective-permute-done.2.three_ref) | copy-start | bytes 196612

commit v2 on v1

--- a/solution.py
+++ b/solution.py
@@ -4,6 +4,7 @@
 from jax.experimental import pallas as pl
 from jax.experimental.pallas import tpu as pltpu
 from jax.sharding import PartitionSpec as P
+
 
 LO = 256
 BLOCK = 1024
@@ -272,12 +273,15 @@
     part_ref[...] = jnp.where(lane == 0, roc[None], jnp.where(lane == 1, prc[None], flag[None]))
 
 
-def join_kernel(own_ref, one_ref, two_ref, three_ref, part_ref, tpr_ref, precision_ref, roc_ref, prc_ref, flag_ref):
+def join_kernel(own_ref, one_ref, two_ref, three_ref, tpr_ref, precision_ref):
     me = lax.axis_index("grp")
     for k, ref in enumerate((own_ref, one_ref, two_ref, three_ref)):
         source = (me - k) & 3
         tpr_ref[source] = ref[0]
         precision_ref[source] = ref[1]
+
+
+def area_kernel(part_ref, roc_ref, prc_ref, flag_ref):
     sums = jnp.sum(part_ref[...].reshape(RANGES, LANES), axis=0, keepdims=True)
     lane = iota((1, LANES), 1)
     roc_ref[0] = jnp.sum(jnp.where(lane == 0, sums, 0.0))
@@ -297,11 +301,19 @@
     return jax.ShapeDtypeStruct(shape, jnp.float32)
 
 
+def near(*shape):
+    return pltpu.VMEM(shape, jnp.float32)
+
+
+def at_hand(x):
+    return pltpu.with_memory_space_constraint(x, pltpu.VMEM)
+
+
 def on_device(bucket, label, group, group_weight):
     blocks = bucket.shape[0] // LANES
     message = pl.pallas_call(
         route_kernel,
-        out_shape=f32(4 * RANGES, LANES),
+        out_shape=near(4 * RANGES, LANES),
         in_specs=[smem(), vmem(), vmem(), vmem()],
         out_specs=vmem(),
         scratch_shapes=[pltpu.VMEM((blocks, LANES), jnp.float32)] * 5
@@ -314,21 +326,28 @@
     received = lax.all_to_all(message.reshape(RANGES, 4, LANES), AXES, 0, 0, tiled=True)
     curves, parts = pl.pallas_call(
         curve_kernel,
-        out_shape=(f32(2, ROWS, LANES), f32(RANGES, 1, LANES)),
+        out_shape=(near(2, ROWS, LANES), near(RANGES, 1, LANES)),
         in_specs=[vmem()],
         out_specs=(vmem(), vmem()),
         scratch_shapes=[pltpu.VMEM((2 * ROWS, 8 * LANES), jnp.bfloat16), pltpu.VMEM((LANES, 8 * LANES), jnp.bfloat16)],
         name="curve",
-    )(received.reshape(4 * RANGES, LANES))
+    )(at_hand(received.reshape(4 * RANGES, LANES)))
+    parts = lax.all_to_all(parts, AXES, 0, 0, tiled=True)
     others = [lax.ppermute(curves, "grp", [(i, (i + k) % 4) for i in range(4)]) for k in (1, 2, 3)]
-    parts = lax.all_to_all(parts, AXES, 0, 0, tiled=True)
-    tpr, precision, roc, prc, flag = pl.pallas_call(
+    tpr, precision = pl.pallas_call(
         join_kernel,
-        out_shape=(f32(4, ROWS, LANES), f32(4, ROWS, LANES), f32(1), f32(1), f32(1)),
-        in_specs=[vmem()] * 5,
-        out_specs=(vmem(), vmem(), smem(), smem(), smem()),
+        out_shape=(f32(4, ROWS, LANES), f32(4, ROWS, LANES)),
+        in_specs=[vmem()] * 4,
+        out_specs=(vmem(), vmem()),
         name="join",
-    )(curves, *others, parts)
+    )(at_hand(curves), *[at_hand(x) for x in others])
+    roc, prc, flag = pl.pallas_call(
+        area_kernel,
+        out_shape=(f32(1), f32(1), f32(1)),
+        in_specs=[vmem()],
+        out_specs=(smem(), smem(), smem()),
+        name="area",
+    )(at_hand(parts))
     quick = (tpr.reshape(4 * ROWS * LANES), precision.reshape(4 * ROWS * LANES), roc.reshape(()), prc.reshape(()))
 
     def again(state):

time: 60.3 us -> 55.7 us (0.924)
  Pallas kernels: 15 us -> 12.5 us
  local copies, waits for them, and re-layouts: 1.25 us -> 0.02 us
  blocking collectives: 38.6 us -> 37.8 us
    pallas_call x2 -> x3, Pallas kernels: 13.3 us -> 11.8 us  [the longest x1 5.94 us: on_device(): pl.pallas_call(route_kernel, out_shape=near(4 * RANGES, LANES), in_specs=...]
    unnamed x14 -> x8, local copies, waits for them, and re-layouts: 1.25 us -> 0.02 us
    pallas_call x1, Pallas kernels: 1.72 us -> 0.73 us  [on_device(): pl.pallas_call(join_kernel, out_shape=(f32(4, ROWS, LANES), f32(4, ROWS,...]
  transfers between devices with their start and end apart: 3 -> 3, of which waited for: 0 -> 0; matrix products, arithmetic and copies ran while one was open for 0% -> 0% of each run, Pallas kernels for 0% -> 1%
where the time goes in v2:
time: 55.7 us; the launch traced here: 55.5 us
  blocking collectives  37.8 us (68%)
  Pallas kernels  12.5 us (22%)
  starting transfers between devices  3.38 us (6%)
  loops' own time  0.92 us (2%)
  between operations  0.91 us (2%)
    all_to_all x1, blocking collectives, on_device(): lax.all_to_all(message.reshape(RANGES, 4, LANES), AXES, 0, 0, tiled=True)  22.2 us
    all_to_all x1, blocking collectives, on_device(): parts = lax.all_to_all(parts, AXES, 0, 0, tiled=True)  15.6 us
    pallas_call x1, Pallas kernels, on_device(): pl.pallas_call(route_kernel, out_shape=near(4 * RANGES, LANES), in_specs=...  5.94 us
    pallas_call x1, Pallas kernels, on_device(): pl.pallas_call(curve_kernel, out_shape=(near(2, ROWS, LANES), near(RANGES...  5.12 us
    ppermute x3, starting transfers between devices, on_device(): lax.ppermute(curves, 'grp', [(i, (i + k) % 4) for i in range(4)])  3.38 us
  transfers between devices with their start and end apart: 3, of which 0 were waited for; matrix products, arithmetic and copies ran while one was open for 0% of the time, Pallas kernels for 1%

profile of v2, /device:TPU:1, one launch (start us, length us, event | category | flops | bytes accessed | tf_op | source)
XLA Modules:
  0.0 55.5 jit_solution(938411575135331764)
XLA Ops:
  0.6 0.0 copy-start
  0.6 0.0 copy-start.1
  0.7 0.0 copy-start.2
  0.7 0.0 copy-start.3
  0.7 5.9 %route.1 = f32[512,128]{1,0:T(8,128)S(1)} custom-call(f32[16]{0:T(128)} %weights_ref.1, s32[48,128]{1,0:T(8,128)} %bitcast.77, s32[48,128]{1,0:T(8,128)} %bitcast.78, s32[48,128]{1,0:T(8,128)} %bitcast.79), custom_call_target="tpu_custom_call" | custom-call | tf_op jit(solution)/shard_map/route/pallas_call | solution.py:314
  6.6 22.2 %all_to_all.23 = f32[128,4,128]{2,1,0:T(4,128)S(1)} all-to-all(f32[128,4,128]{2,1,0:T(4,128)S(1)} %bitcast.73), channel_id=1, replica_groups=mesh['grp'=4,'shard'=32] {'grp','shard'}, dimensions={0} | all-to-all | bytes 524288 | tf_op jit(solution)/shard_map/all_to_all | solution.py:326
  28.8 5.1 %curve.1 = (f32[2,64,128]{2,1,0:T(8,128)S(1)}, f32[128,1,128]{2,1,0:T(1,128)S(1)}) custom-call(f32[512,128]{1,0:T(8,128)S(1)} %bitcast.72), custom_call_target="tpu_custom_call" | custom-call | tf_op jit(solution)/shard_map/curve/pallas_call | solution.py:327
  33.9 0.3 collective-permute-start
  34.3 1.7 %collective-permute-start.1 = (f32[2,64,128]{2,1,0:T(8,128)S(1)}, f32[2,64,128]{2,1,0:T(8,128)S(1)}, u32[]{:S(2)}, u32[]{:S(2)}) collective-permute-start(f32[2,64,128]{2,1,0:T(8,128)S(1)} %get-tuple-element.138.own_ref), channel_id=1, source_target_pairs={{0,64},{32,96},{64,0},{96,32},{1,65},{33,97},{65,1},{97,33},{2,66}... | collective-permute-start | bytes 196616 | tf_op jit(solution)/shard_map/ppermute | solution.py:336
  35.9 1.4 %collective-permute-start.2 = (f32[2,64,128]{2,1,0:T(8,128)S(1)}, f32[2,64,128]{2,1,0:T(8,128)S(1)}, u32[]{:S(2)}, u32[]{:S(2)}) collective-permute-start(f32[2,64,128]{2,1,0:T(8,128)S(1)} %get-tuple-element.138.own_ref), channel_id=1, source_target_pairs={{0,96},{32,0},{64,32},{96,64},{1,97},{33,1},{65,33},{97,65},{2,98}... | collective-permute-start | bytes 196616 | tf_op jit(solution)/shard_map/ppermute | solution.py:336
  37.3 15.6 %all_to_all.24.part_ref = f32[128,1,128]{2,1,0:T(1,128)S(1)} all-to-all(f32[128,1,128]{2,1,0:T(1,128)S(1)} %get-tuple-element.136), channel_id=1, replica_groups=mesh['grp'=4,'shard'=32] {'grp','shard'}, dimensions={0} | all-to-all | bytes 131072 | tf_op jit(solution)/shard_map/all_to_all | solution.py:335
  52.9 0.7 %area.1 = (f32[1]{0:T(128)}, f32[1]{0:T(128)}, f32[1]{0:T(128)}) custom-call(f32[128,1,128]{2,1,0:T(1,128)S(1)} %all_to_all.24.part_ref), custom_call_target="tpu_custom_call" | custom-call | tf_op jit(solution)/shard_map/area/pallas_call | solution.py:344
  53.6 0.0 collective-permute-done.one_ref
  53.6 0.0 collective-permute-done.1.two_ref
  53.7 0.0 collective-permute-done.2.three_ref
  53.7 0.7 %join.1 = (f32[4,64,128]{2,1,0:T(8,128)}, f32[4,64,128]{2,1,0:T(8,128)}) custom-call(f32[2,64,128]{2,1,0:T(8,128)S(1)} %get-tuple-element.138.own_ref, f32[2,64,128]{2,1,0:T(8,128)S(1)} %collective-permute-done.one_ref, f32[2,64,128]{2,1,0:T(8,128)S(1)} %collective-permute-done.1.two_ref, f32[2,64,128]{2,1,0:T(8,128)S(1)} %collective-permute-done.2.three_ref), custom_call_target="tpu_custom_call" | custom-call | tf_op jit(solution)/shard_map/join/pallas_call | solution.py:337
  54.4 0.0 copy-done
  54.4 0.0 copy-done.1
  54.4 0.0 copy-done.2
  54.4 0.0 copy-done.3
  54.4 0.9 %while.26 = (f32[]{:T(128)}, f32[32768]{0:T(1024)}, f32[32768]{0:T(1024)}, f32[]{:T(128)}, f32[]{:T(128)}, /*index=5*/s32[6144]{0:T(1024)S(1)}, s32[6144]{0:T(1024)S(1)}, f32[16]{0:T(128)S(1)}, s32[6144]{0:T(1024)S(1)}) while((f32[]{:T(128)}, f32[32768]{0:T(1024)}, f32[32768]{0:T(1024)}, f32[]{:T(128)}, f32[]{:T(128)}, /*index=5*/s32[6144]{0:T(1024)S(1)}, ...), condition=%region_12.13_spmd, body=%region_0.12_spmd | while | flops 349572256 | bytes 22732732 | solution.py:356
Async XLA Ops:
  0.6 53.8 %copy-start = (s32[6144]{0:T(1024)S(1)}, s32[6144]{0:T(1024)}, u32[]{:S(2)}) copy-start(s32[6144]{0:T(1024)} %param.8) | copy-start | bytes 73732
  0.6 53.8 %copy-start.1 = (s32[6144]{0:T(1024)S(1)}, s32[6144]{0:T(1024)}, u32[]{:S(2)}) copy-start(s32[6144]{0:T(1024)} %param.9) | copy-start | bytes 73732
  0.7 53.8 %copy-start.2 = (s32[6144]{0:T(1024)S(1)}, s32[6144]{0:T(1024)}, u32[]{:S(2)}) copy-start(s32[6144]{0:T(1024)} %param.10) | copy-start | bytes 73732
  0.7 53.7 %copy-start.3 = (f32[16]{0:T(128)S(1)}, f32[16]{0:T(128)}, u32[]{:S(2)}) copy-start(f32[16]{0:T(128)} %weights_ref.1) | copy-start | bytes 196
  33.9 19.7 %collective-permute-start = (f32[2,64,128]{2,1,0:T(8,128)S(1)}, f32[2,64,128]{2,1,0:T(8,128)S(1)}, u32[]{:S(2)}, u32[]{:S(2)}) collective-permute-start(f32[2,64,128]{2,1,0:T(8,128)S(1)} %get-tuple-element.138.own_ref), channel_id=1, source_target_pairs={{0,32},{32,64},{64,96},{96,0},{1,33},{33,65},{65,97},{97,1},{2,34}... | collective-permute-start | bytes 196616 | tf_op jit(solution)/shard_map/ppermute | solution.py:336
  34.3 19.4 %collective-permute-start.1 = (f32[2,64,128]{2,1,0:T(8,128)S(1)}, f32[2,64,128]{2,1,0:T(8,128)S(1)}, u32[]{:S(2)}, u32[]{:S(2)}) collective-permute-start(f32[2,64,128]{2,1,0:T(8,128)S(1)} %get-tuple-element.138.own_ref), channel_id=1, source_target_pairs={{0,64},{32,96},{64,0},{96,32},{1,65},{33,97},{65,1},{97,33},{2,66}... | collective-permute-start | bytes 196616 | tf_op jit(solution)/shard_map/ppermute | solution.py:336
  35.9 17.7 %collective-permute-start.2 = (f32[2,64,128]{2,1,0:T(8,128)S(1)}, f32[2,64,128]{2,1,0:T(8,128)S(1)}, u32[]{:S(2)}, u32[]{:S(2)}) collective-permute-start(f32[2,64,128]{2,1,0:T(8,128)S(1)} %get-tuple-element.138.own_ref), channel_id=1, source_target_pairs={{0,96},{32,0},{64,32},{96,64},{1,97},{33,1},{65,33},{97,65},{2,98}... | collective-permute-start | bytes 196616 | tf_op jit(solution)/shard_map/ppermute | solution.py:336

commit v3 on v2

--- a/solution.py
+++ b/solution.py
@@ -129,116 +129,124 @@
     return jnp.broadcast_to(row, (16, row.shape[1])).astype(jnp.bfloat16)
 
 
+def one_hot(row, groups, value, none):
+    first = iota((16, LANES), 0).astype(jnp.float32).astype(jnp.bfloat16)
+    return [jnp.where(first + jnp.bfloat16(16 * k) == row, value, none) for k in range(groups)]
+
+
 def route_kernel(weights_ref, bucket_ref, label_ref, group_ref, out_ref,
-                 peer_s, high_s, low_s, pos_s, neg_s, one_s, left_s, right_s, acc_s):
+                 peer_s, high_s, low_s, sign_s, part_s, acc_s):
     blocks = bucket_ref.shape[0]
-    step = 8
+    step = 48
     bucket = bucket_ref[...]
     group = group_ref[...]
     weight = jnp.zeros(group.shape, jnp.float32)
     for k in range(weights_ref.shape[0]):
         weight = jnp.where(group == k, weights_ref[k], weight)
     labels = label_ref[...].astype(jnp.float32)
-    pos_s[...] = weight * labels
-    neg_s[...] = weight * (1.0 - labels)
+    positive = (weight * labels).astype(jnp.bfloat16).astype(jnp.float32)
+    negative = (weight * (1.0 - labels)).astype(jnp.bfloat16).astype(jnp.float32)
+    sign_s[...] = positive - negative
     which = bucket >> RANGE_BITS
     peer = ((which & 3) << 5) | (which >> 2)
     peer_s[...] = peer.astype(jnp.float32)
     high_s[...] = ((bucket >> 7) & (ROWS - 1)).astype(jnp.float32)
     low_s[...] = (bucket & (LANES - 1)).astype(jnp.float32)
 
-    before = (iota((LANES, 2 * LANES), 0) < iota((LANES, 2 * LANES), 1)).astype(jnp.bfloat16)
-    sub = iota((16, LANES), 0)
+    wide = 2 * LANES
+    upto = (iota((wide, wide), 0) <= iota((wide, wide), 1)).astype(jnp.bfloat16)
+    none = jnp.zeros((16, LANES), jnp.bfloat16)
     unit = jnp.ones((16, LANES), jnp.bfloat16)
-    none = jnp.zeros((16, LANES), jnp.bfloat16)
-    kind = sub & 3
-    sub_f = sub.astype(jnp.float32).astype(jnp.bfloat16)
-    quarter_f = (sub >> 2).astype(jnp.float32).astype(jnp.bfloat16)
     acc_s[...] = jnp.zeros(acc_s.shape, jnp.float32)
 
     def chunk(i, count):
+        ones = []
         for u in range(step):
             row = bf16_rows(peer_s[pl.ds(i * step + u, 1), :])
-            for k in range(8):
-                one_s[pl.ds(u * LANES + 16 * k, 16), :] = jnp.where(
-                    sub_f + jnp.bfloat16(16 * k) == row, unit, none)
-        ones = one_s[...]
-        seen = lax.dot_general(ones, before, NN, preferred_element_type=jnp.float32)
-        for u in range(step):
-            mine = ones[u * LANES:(u + 1) * LANES].astype(jnp.float32)
-            part = seen[u * LANES:(u + 1) * LANES]
-            rank = jnp.sum(mine * (part[:, :LANES] + count), axis=0, keepdims=True)
-            count = count + part[:, LANES:]
-            j = i * step + u
-            lanes = pl.ds(u * LANES, LANES)
-            rank_row = bf16_rows(jnp.minimum(rank, 255.0))
-            for k in range(8):
-                right_s[pl.ds(16 * k, 16), lanes] = jnp.where(
-                    sub_f + jnp.bfloat16(16 * k) == rank_row, unit, none)
-            high = jnp.broadcast_to(high_s[pl.ds(j, 1), :], (16, LANES))
-            low = jnp.broadcast_to(low_s[pl.ds(j, 1), :], (16, LANES))
-            pos = jnp.broadcast_to(pos_s[pl.ds(j, 1), :], (16, LANES))
-            neg = jnp.broadcast_to(neg_s[pl.ds(j, 1), :], (16, LANES))
-            value = jnp.where(kind == 0, high, jnp.where(kind == 1, low, jnp.where(kind == 2, pos, neg)))
-            value = value.astype(jnp.bfloat16)
-            row = bf16_rows(peer_s[pl.ds(j, 1), :])
-            for k in range(32):
-                left_s[pl.ds(16 * k, 16), lanes] = jnp.where(
-                    quarter_f + jnp.bfloat16(4 * k) == row, value, none)
-        acc_s[...] += lax.dot_general(left_s[...], right_s[...], NT, preferred_element_type=jnp.float32)
+            ones.append(jnp.concatenate(one_hot(row, 8, unit, none), axis=0))
+        for v in range(step // 2):
+            pair = jnp.concatenate([ones[2 * v], ones[2 * v + 1]], axis=1)
+            seen = lax.dot_general(pair, upto, NN, preferred_element_type=jnp.float32)
+            for h in range(2):
+                u = 2 * v + h
+                mine = ones[u].astype(jnp.float32)
+                before = seen[:, h * LANES:(h + 1) * LANES] + count
+                rank = jnp.sum(mine * before, axis=0, keepdims=True) - 1.0
+                rank = bf16_rows(jnp.minimum(rank, 255.0))
+                j = i * step + u
+                high = bf16_rows(high_s[pl.ds(j, 1), :])
+                low = bf16_rows(low_s[pl.ds(j, 1), :])
+                sign = bf16_rows(sign_s[pl.ds(j, 1), :])
+                first = iota((16, LANES), 0).astype(jnp.float32).astype(jnp.bfloat16)
+                for k in range(8):
+                    same = first + jnp.bfloat16(16 * k) == rank
+                    part_s[u, pl.ds(16 * k, 16), :] = jnp.where(same, high, none)
+                    part_s[u, pl.ds(LANES + 16 * k, 16), :] = jnp.where(same, low, none)
+                    part_s[u, pl.ds(2 * LANES + 16 * k, 16), :] = jnp.where(same, sign, none)
+            count = count + jnp.broadcast_to(seen[:, wide - 1:wide], (RANGES, LANES))
+        left = jnp.concatenate([part_s[u] for u in range(step)], axis=1)
+        right = jnp.concatenate(ones, axis=1)
+        acc_s[...] += lax.dot_general(left, right, NT, preferred_element_type=jnp.float32)
         return count
 
     count = lax.fori_loop(0, blocks // step, chunk, jnp.zeros((RANGES, LANES), jnp.float32))
     full = jnp.max(jnp.where(count > CAP, 1.0, 0.0), axis=0, keepdims=True)
     full = jnp.max(full, axis=1, keepdims=True)
 
-    lane = iota((RANGES, LANES), 1)
-    real = lane < CAP
-    high = acc_s[pl.ds(0, RANGES, stride=4), :]
-    low = acc_s[pl.ds(1, RANGES, stride=4), :]
-    pos = jnp.where(real, acc_s[pl.ds(2, RANGES, stride=4), :], 0.0)
-    neg = jnp.where(real, acc_s[pl.ds(3, RANGES, stride=4), :], 0.0)
+    slot = iota((LANES, RANGES), 0)
+    real = slot < CAP
+    high = acc_s[pl.ds(0, LANES), :]
+    low = acc_s[pl.ds(LANES, LANES), :]
+    sign = jnp.where(real, acc_s[pl.ds(2 * LANES, LANES), :], 0.0)
+    pos = jnp.maximum(sign, 0.0)
+    neg = jnp.maximum(-sign, 0.0)
     p0 = iota((RANGES, RANGES), 0)
     p1 = iota((RANGES, RANGES), 1)
     r0 = ((p0 & 31) << 2) | (p0 >> 5)
     r1 = ((p1 & 31) << 2) | (p1 >> 5)
-    above = (r1 > r0).astype(jnp.bfloat16)
-    both = jnp.concatenate([pos, neg], axis=1).astype(jnp.bfloat16)
-    later = lax.dot_general(above, both, NN, preferred_element_type=jnp.float32)
-    higher_pos = jnp.sum(later[:, :LANES], axis=1, keepdims=True)
-    higher_neg = jnp.sum(later[:, LANES:], axis=1, keepdims=True)
-    total_pos = jnp.sum(jnp.sum(pos, axis=0, keepdims=True), axis=1, keepdims=True)
-    total_neg = jnp.sum(jnp.sum(neg, axis=0, keepdims=True), axis=1, keepdims=True)
-    out_ref[pl.ds(0, RANGES, stride=4), :] = jnp.where(real, high, full)
-    out_ref[pl.ds(1, RANGES, stride=4), :] = low
-    out_ref[pl.ds(2, RANGES, stride=4), :] = jnp.where(real, pos, jnp.where(lane == CAP, higher_pos, total_pos))
-    out_ref[pl.ds(3, RANGES, stride=4), :] = jnp.where(real, neg, jnp.where(lane == CAP, higher_neg, total_neg))
-
-
-def curve_kernel(in_ref, curve_ref, part_ref, left_s, right_s):
-    step = 8
-    sub_f = iota((16, LANES), 0).astype(jnp.float32).astype(jnp.bfloat16)
+    above = (r0 > r1).astype(jnp.bfloat16)
+    both = jnp.concatenate([pos, neg], axis=0).astype(jnp.bfloat16)
+    later = lax.dot_general(both, above, NN, preferred_element_type=jnp.float32)
+    for c, own in ((2, pos), (3, neg)):
+        higher = jnp.sum(later[(c - 2) * LANES:(c - 1) * LANES], axis=0, keepdims=True)
+        total = jnp.sum(jnp.sum(own, axis=0, keepdims=True), axis=1, keepdims=True)
+        sent = jnp.where(real, own, jnp.where(slot == CAP, higher, total))
+        out_ref[pl.ds(c, RANGES, stride=4), :] = sent.T
+    out_ref[pl.ds(0, RANGES, stride=4), :] = jnp.where(real, high, full).T
+    out_ref[pl.ds(1, RANGES, stride=4), :] = low.T
+
+
+def in_three(x):
+    first = x.astype(jnp.bfloat16)
+    rest = x - first.astype(jnp.float32)
+    second = rest.astype(jnp.bfloat16)
+    rest = rest - second.astype(jnp.float32)
+    return first, second, rest.astype(jnp.bfloat16)
+
+
+def curve_kernel(in_ref, curve_ref, part_ref):
+    step = 128
     none = jnp.zeros((16, LANES), jnp.bfloat16)
     unit = jnp.ones((16, LANES), jnp.bfloat16)
-    real = iota((1, LANES), 1) < CAP
+    first = iota((16, LANES), 0).astype(jnp.float32).astype(jnp.bfloat16)
+    real = iota((16, LANES), 1) < CAP
 
     def chunk(i, carry):
         hist, sums = carry
+        left = []
+        right = []
         for u in range(step):
             at = (i * step + u) * 4
-            lanes = pl.ds(u * LANES, LANES)
             high = bf16_rows(in_ref[pl.ds(at, 1), :])
             low = bf16_rows(in_ref[pl.ds(at + 1, 1), :])
-            pos = bf16_rows(jnp.where(real, in_ref[pl.ds(at + 2, 1), :], 0.0))
-            neg = bf16_rows(jnp.where(real, in_ref[pl.ds(at + 3, 1), :], 0.0))
-            for k in range(4):
-                same = sub_f + jnp.bfloat16(16 * k) == high
-                left_s[pl.ds(16 * k, 16), lanes] = jnp.where(same, pos, none)
-                left_s[pl.ds(ROWS + 16 * k, 16), lanes] = jnp.where(same, neg, none)
-            for k in range(8):
-                right_s[pl.ds(16 * k, 16), lanes] = jnp.where(
-                    sub_f + jnp.bfloat16(16 * k) == low, unit, none)
-        hist = hist + lax.dot_general(left_s[...], right_s[...], NT, preferred_element_type=jnp.float32)
+            pos = jnp.where(real, jnp.broadcast_to(in_ref[pl.ds(at + 2, 1), :], (16, LANES)), 0.0).astype(jnp.bfloat16)
+            neg = jnp.where(real, jnp.broadcast_to(in_ref[pl.ds(at + 3, 1), :], (16, LANES)), 0.0).astype(jnp.bfloat16)
+            same = [first + jnp.bfloat16(16 * k) == high for k in range(4)]
+            left.append(jnp.concatenate(
+                [jnp.where(m, pos, none) for m in same] + [jnp.where(m, neg, none) for m in same], axis=0))
+            right.append(jnp.concatenate(one_hot(low, 8, unit, none), axis=0))
+        hist = hist + lax.dot_general(jnp.concatenate(left, axis=1), jnp.concatenate(right, axis=1), NT,
+                                      preferred_element_type=jnp.float32)
         for u in range(step // 2):
             sums = sums + in_ref[pl.ds((i * step + 2 * u) * 4, 8), :]
         return hist, sums
@@ -251,12 +259,15 @@
     total_pos = sums[2:3, CAP + 1:CAP + 2]
     higher_neg = sums[3:4, CAP:CAP + 1]
     total_neg = sums[3:4, CAP + 1:CAP + 2]
-    upper = (iota((LANES, LANES), 0) >= iota((LANES, LANES), 1)).astype(jnp.float32)
+    upper = (iota((LANES, LANES), 0) >= iota((LANES, LANES), 1)).astype(jnp.bfloat16)
     row = iota((2 * ROWS, 2 * ROWS), 0)
     col = iota((2 * ROWS, 2 * ROWS), 1)
-    below = ((col > row) & ((col >= ROWS) == (row >= ROWS))).astype(jnp.float32)
-    in_row = lax.dot_general(hist, upper, NN, precision=HIGHEST, preferred_element_type=jnp.float32)
-    rows_after = lax.dot_general(below, hist, NN, precision=HIGHEST, preferred_element_type=jnp.float32)
+    below = ((col > row) & ((col >= ROWS) == (row >= ROWS))).astype(jnp.bfloat16)
+    pieces = in_three(hist)
+    in_row = lax.dot_general(jnp.concatenate(pieces, axis=1), jnp.concatenate([upper] * 3, axis=0), NN,
+                             preferred_element_type=jnp.float32)
+    rows_after = lax.dot_general(jnp.concatenate([below] * 3, axis=1), jnp.concatenate(pieces, axis=0), NN,
+                                 preferred_element_type=jnp.float32)
     cumulative = in_row + jnp.sum(rows_after, axis=1, keepdims=True)
     true_pos = cumulative[:ROWS] + higher_pos
     false_pos = cumulative[ROWS:] + higher_neg
@@ -316,11 +327,8 @@
         out_shape=near(4 * RANGES, LANES),
         in_specs=[smem(), vmem(), vmem(), vmem()],
         out_specs=vmem(),
-        scratch_shapes=[pltpu.VMEM((blocks, LANES), jnp.float32)] * 5
-        + [pltpu.VMEM((8 * LANES, LANES), jnp.bfloat16),
-           pltpu.VMEM((4 * RANGES, 8 * LANES), jnp.bfloat16),
-           pltpu.VMEM((LANES, 8 * LANES), jnp.bfloat16),
-           pltpu.VMEM((4 * RANGES, LANES), jnp.float32)],
+        scratch_shapes=[pltpu.VMEM((blocks, LANES), jnp.float32)] * 4
+        + [pltpu.VMEM((48, 3 * LANES, LANES), jnp.bfloat16), pltpu.VMEM((3 * LANES, LANES), jnp.float32)],
         name="route",
     )(group_weight, bucket.reshape(blocks, LANES), label.reshape(blocks, LANES), group.reshape(blocks, LANES))
     received = lax.all_to_all(message.reshape(RANGES, 4, LANES), AXES, 0, 0, tiled=True)
@@ -329,7 +337,6 @@
         out_shape=(near(2, ROWS, LANES), near(RANGES, 1, LANES)),
         in_specs=[vmem()],
         out_specs=(vmem(), vmem()),
-        scratch_shapes=[pltpu.VMEM((2 * ROWS, 8 * LANES), jnp.bfloat16), pltpu.VMEM((LANES, 8 * LANES), jnp.bfloat16)],
         name="curve",
     )(at_hand(received.reshape(4 * RANGES, LANES)))
     parts = lax.all_to_all(parts, AXES, 0, 0, tiled=True)

time: 55.7 us -> 50 us (0.90)
  Pallas kernels: 12.5 us -> 6.79 us
    pallas_call x1, Pallas kernels: 5.12 us -> 1.78 us  [on_device(): pl.pallas_call(curve_kernel, out_shape=(near(2, ROWS, LANES), near(RANGES...]
    pallas_call x1, Pallas kernels: 5.94 us -> 3.56 us  [on_device(): pl.pallas_call(route_kernel, out_shape=near(4 * RANGES, LANES), in_specs=...]
where the time goes in v3:
time: 50 us; the launch traced here: 49.8 us
  blocking collectives  37.8 us (76%)
  Pallas kernels  6.79 us (14%)
  starting transfers between devices  3.37 us (7%)
  loops' own time  0.92 us (2%)
  between operations  0.91 us (2%)
    all_to_all x1, blocking collectives, on_device(): lax.all_to_all(message.reshape(RANGES, 4, LANES), AXES, 0, 0, tiled=True)  22.2 us
    all_to_all x1, blocking collectives, on_device(): parts = lax.all_to_all(parts, AXES, 0, 0, tiled=True)  15.6 us
    pallas_call x1, Pallas kernels, on_device(): pl.pallas_call(route_kernel, out_shape=near(4 * RANGES, LANES), in_specs=...  3.56 us
    ppermute x3, starting transfers between devices, on_device(): lax.ppermute(curves, 'grp', [(i, (i + k) % 4) for i in range(4)])  3.37 us
    pallas_call x1, Pallas kernels, on_device(): pl.pallas_call(curve_kernel, out_shape=(near(2, ROWS, LANES), near(RANGES...  1.78 us
  transfers between devices with their start and end apart: 3, of which 0 were waited for; matrix products, arithmetic and copies ran while one was open for 0% of the time, Pallas kernels for 1%

profile of v3, /device:TPU:1, one launch (start us, length us, event | category | flops | bytes accessed | tf_op | source)
XLA Modules:
  0.0 49.8 jit_solution(2221586721404755996)
XLA Ops:
  0.6 0.0 copy-start
  0.6 0.0 copy-start.1
  0.7 0.0 copy-start.2
  0.7 0.0 copy-start.3
  0.7 3.6 %route.1 = f32[512,128]{1,0:T(8,128)S(1)} custom-call(f32[16]{0:T(128)} %weights_ref.1, s32[48,128]{1,0:T(8,128)} %bitcast.77, s32[48,128]{1,0:T(8,128)} %bitcast.78, s32[48,128]{1,0:T(8,128)} %bitcast.79), custom_call_target="tpu_custom_call" | custom-call | tf_op jit(solution)/shard_map/route/pallas_call | solution.py:325
  4.2 22.2 %all_to_all.23 = f32[128,4,128]{2,1,0:T(4,128)S(1)} all-to-all(f32[128,4,128]{2,1,0:T(4,128)S(1)} %bitcast.73), channel_id=1, replica_groups=mesh['grp'=4,'shard'=32] {'grp','shard'}, dimensions={0} | all-to-all | bytes 524288 | tf_op jit(solution)/shard_map/all_to_all | solution.py:334
  26.4 1.8 %curve.1 = (f32[2,64,128]{2,1,0:T(8,128)S(1)}, f32[128,1,128]{2,1,0:T(1,128)S(1)}) custom-call(f32[512,128]{1,0:T(8,128)S(1)} %bitcast.72), custom_call_target="tpu_custom_call" | custom-call | tf_op jit(solution)/shard_map/curve/pallas_call | solution.py:335
  28.2 0.3 collective-permute-start
  28.5 1.7 %collective-permute-start.1 = (f32[2,64,128]{2,1,0:T(8,128)S(1)}, f32[2,64,128]{2,1,0:T(8,128)S(1)}, u32[]{:S(2)}, u32[]{:S(2)}) collective-permute-start(f32[2,64,128]{2,1,0:T(8,128)S(1)} %get-tuple-element.138.own_ref), channel_id=1, source_target_pairs={{0,64},{32,96},{64,0},{96,32},{1,65},{33,97},{65,1},{97,33},{2,66}... | collective-permute-start | bytes 196616 | tf_op jit(solution)/shard_map/ppermute | solution.py:343
  30.2 1.4 %collective-permute-start.2 = (f32[2,64,128]{2,1,0:T(8,128)S(1)}, f32[2,64,128]{2,1,0:T(8,128)S(1)}, u32[]{:S(2)}, u32[]{:S(2)}) collective-permute-start(f32[2,64,128]{2,1,0:T(8,128)S(1)} %get-tuple-element.138.own_ref), channel_id=1, source_target_pairs={{0,96},{32,0},{64,32},{96,64},{1,97},{33,1},{65,33},{97,65},{2,98}... | collective-permute-start | bytes 196616 | tf_op jit(solution)/shard_map/ppermute | solution.py:343
  31.6 15.6 %all_to_all.24.part_ref = f32[128,1,128]{2,1,0:T(1,128)S(1)} all-to-all(f32[128,1,128]{2,1,0:T(1,128)S(1)} %get-tuple-element.136), channel_id=1, replica_groups=mesh['grp'=4,'shard'=32] {'grp','shard'}, dimensions={0} | all-to-all | bytes 131072 | tf_op jit(solution)/shard_map/all_to_all | solution.py:342
  47.2 0.7 %area.1 = (f32[1]{0:T(128)}, f32[1]{0:T(128)}, f32[1]{0:T(128)}) custom-call(f32[128,1,128]{2,1,0:T(1,128)S(1)} %all_to_all.24.part_ref), custom_call_target="tpu_custom_call" | custom-call | tf_op jit(solution)/shard_map/area/pallas_call | solution.py:351
  47.9 0.0 collective-permute-done.one_ref
  47.9 0.0 collective-permute-done.1.two_ref
  47.9 0.0 collective-permute-done.2.three_ref
  47.9 0.7 %join.1 = (f32[4,64,128]{2,1,0:T(8,128)}, f32[4,64,128]{2,1,0:T(8,128)}) custom-call(f32[2,64,128]{2,1,0:T(8,128)S(1)} %get-tuple-element.138.own_ref, f32[2,64,128]{2,1,0:T(8,128)S(1)} %collective-permute-done.one_ref, f32[2,64,128]{2,1,0:T(8,128)S(1)} %collective-permute-done.1.two_ref, f32[2,64,128]{2,1,0:T(8,128)S(1)} %collective-permute-done.2.three_ref), custom_call_target="tpu_custom_call" | custom-call | tf_op jit(solution)/shard_map/join/pallas_call | solution.py:344
  48.7 0.0 copy-done
  48.7 0.0 copy-done.1
  48.7 0.0 copy-done.2
  48.7 0.0 copy-done.3
  48.7 0.9 %while.26 = (f32[]{:T(128)}, f32[32768]{0:T(1024)}, f32[32768]{0:T(1024)}, f32[]{:T(128)}, f32[]{:T(128)}, /*index=5*/s32[6144]{0:T(1024)S(1)}, s32[6144]{0:T(1024)S(1)}, f32[16]{0:T(128)S(1)}, s32[6144]{0:T(1024)S(1)}) while((f32[]{:T(128)}, f32[32768]{0:T(1024)}, f32[32768]{0:T(1024)}, f32[]{:T(128)}, f32[]{:T(128)}, /*index=5*/s32[6144]{0:T(1024)S(1)}, ...), condition=%region_12.13_spmd, body=%region_0.12_spmd | while | flops 349572256 | bytes 22732732 | solution.py:363
Async XLA Ops:
  0.6 48.0 %copy-start = (s32[6144]{0:T(1024)S(1)}, s32[6144]{0:T(1024)}, u32[]{:S(2)}) copy-start(s32[6144]{0:T(1024)} %param.8) | copy-start | bytes 73732
  0.6 48.0 %copy-start.1 = (s32[6144]{0:T(1024)S(1)}, s32[6144]{0:T(1024)}, u32[]{:S(2)}) copy-start(s32[6144]{0:T(1024)} %param.9) | copy-start | bytes 73732
  0.7 48.0 %copy-start.2 = (s32[6144]{0:T(1024)S(1)}, s32[6144]{0:T(1024)}, u32[]{:S(2)}) copy-start(s32[6144]{0:T(1024)} %param.10) | copy-start | bytes 73732
  0.7 48.0 %copy-start.3 = (f32[16]{0:T(128)S(1)}, f32[16]{0:T(128)}, u32[]{:S(2)}) copy-start(f32[16]{0:T(128)} %weights_ref.1) | copy-start | bytes 196
  28.2 19.7 %collective-permute-start = (f32[2,64,128]{2,1,0:T(8,128)S(1)}, f32[2,64,128]{2,1,0:T(8,128)S(1)}, u32[]{:S(2)}, u32[]{:S(2)}) collective-permute-start(f32[2,64,128]{2,1,0:T(8,128)S(1)} %get-tuple-element.138.own_ref), channel_id=1, source_target_pairs={{0,32},{32,64},{64,96},{96,0},{1,33},{33,65},{65,97},{97,1},{2,34}... | collective-permute-start | bytes 196616 | tf_op jit(solution)/shard_map/ppermute | solution.py:343
  28.5 19.4 %collective-permute-start.1 = (f32[2,64,128]{2,1,0:T(8,128)S(1)}, f32[2,64,128]{2,1,0:T(8,128)S(1)}, u32[]{:S(2)}, u32[]{:S(2)}) collective-permute-start(f32[2,64,128]{2,1,0:T(8,128)S(1)} %get-tuple-element.138.own_ref), channel_id=1, source_target_pairs={{0,64},{32,96},{64,0},{96,32},{1,65},{33,97},{65,1},{97,33},{2,66}... | collective-permute-start | bytes 196616 | tf_op jit(solution)/shard_map/ppermute | solution.py:343
  30.2 17.7 %collective-permute-start.2 = (f32[2,64,128]{2,1,0:T(8,128)S(1)}, f32[2,64,128]{2,1,0:T(8,128)S(1)}, u32[]{:S(2)}, u32[]{:S(2)}) collective-permute-start(f32[2,64,128]{2,1,0:T(8,128)S(1)} %get-tuple-element.138.own_ref), channel_id=1, source_target_pairs={{0,96},{32,0},{64,32},{96,64},{1,97},{33,1},{65,33},{97,65},{2,98}... | collective-permute-start | bytes 196616 | tf_op jit(solution)/shard_map/ppermute | solution.py:343

commit v4 on v3

--- a/solution.py
+++ b/solution.py
@@ -9,6 +9,7 @@
 LO = 256
 BLOCK = 1024
 HI = 4096
+BATCH = 6
 
 AXES = ("grp", "shard")
 LANES = 128
@@ -135,9 +136,8 @@
 
 
 def route_kernel(weights_ref, bucket_ref, label_ref, group_ref, out_ref,
-                 peer_s, high_s, low_s, sign_s, part_s, acc_s):
+                 peer_s, high_s, low_s, sign_s):
     blocks = bucket_ref.shape[0]
-    step = 48
     bucket = bucket_ref[...]
     group = group_ref[...]
     weight = jnp.zeros(group.shape, jnp.float32)
@@ -157,47 +157,55 @@
     upto = (iota((wide, wide), 0) <= iota((wide, wide), 1)).astype(jnp.bfloat16)
     none = jnp.zeros((16, LANES), jnp.bfloat16)
     unit = jnp.ones((16, LANES), jnp.bfloat16)
-    acc_s[...] = jnp.zeros(acc_s.shape, jnp.float32)
-
-    def chunk(i, count):
-        ones = []
-        for u in range(step):
-            row = bf16_rows(peer_s[pl.ds(i * step + u, 1), :])
-            ones.append(jnp.concatenate(one_hot(row, 8, unit, none), axis=0))
-        for v in range(step // 2):
-            pair = jnp.concatenate([ones[2 * v], ones[2 * v + 1]], axis=1)
-            seen = lax.dot_general(pair, upto, NN, preferred_element_type=jnp.float32)
+
+    first = iota((16, LANES), 0).astype(jnp.float32).astype(jnp.bfloat16)
+    ones = []
+    for j in range(blocks):
+        row = bf16_rows(peer_s[pl.ds(j, 1), :])
+        ones.append(jnp.concatenate(one_hot(row, 8, unit, none), axis=0))
+    pairs = [jnp.concatenate(ones[j:j + 2], axis=1) for j in range(0, blocks, 2)]
+    count = jnp.zeros((RANGES, LANES), jnp.float32)
+    left = []
+    right = []
+    for v in range(0, len(pairs), BATCH):
+        batch = pairs[v:v + BATCH]
+        seen_all = lax.dot_general(jnp.concatenate(batch, axis=0), upto, NN, preferred_element_type=jnp.float32)
+        for w in range(len(batch)):
+            seen = seen_all[w * RANGES:(w + 1) * RANGES]
             for h in range(2):
-                u = 2 * v + h
-                mine = ones[u].astype(jnp.float32)
+                j = 2 * (v + w) + h
+                mine = ones[j].astype(jnp.float32)
                 before = seen[:, h * LANES:(h + 1) * LANES] + count
                 rank = jnp.sum(mine * before, axis=0, keepdims=True) - 1.0
-                rank = bf16_rows(jnp.minimum(rank, 255.0))
-                j = i * step + u
+                upper = rank >= LANES // 2
+                rank = bf16_rows(jnp.where(upper, rank - LANES // 2, rank))
+                upper = bf16_rows(jnp.where(upper, 1.0, 0.0)) > none
                 high = bf16_rows(high_s[pl.ds(j, 1), :])
                 low = bf16_rows(low_s[pl.ds(j, 1), :])
                 sign = bf16_rows(sign_s[pl.ds(j, 1), :])
-                first = iota((16, LANES), 0).astype(jnp.float32).astype(jnp.bfloat16)
-                for k in range(8):
-                    same = first + jnp.bfloat16(16 * k) == rank
-                    part_s[u, pl.ds(16 * k, 16), :] = jnp.where(same, high, none)
-                    part_s[u, pl.ds(LANES + 16 * k, 16), :] = jnp.where(same, low, none)
-                    part_s[u, pl.ds(2 * LANES + 16 * k, 16), :] = jnp.where(same, sign, none)
+                same = [first + jnp.bfloat16(16 * k) == rank for k in range(4)]
+                left.append(jnp.concatenate(
+                    [jnp.where(m, value, none) for value in (high, low, sign) for m in same], axis=0))
+                parts = [ones[j][16 * k:16 * k + 16] for k in range(8)]
+                right.append(jnp.concatenate(
+                    [jnp.where(upper, none, part) for part in parts] + [jnp.where(upper, part, none) for part in parts],
+                    axis=0))
             count = count + jnp.broadcast_to(seen[:, wide - 1:wide], (RANGES, LANES))
-        left = jnp.concatenate([part_s[u] for u in range(step)], axis=1)
-        right = jnp.concatenate(ones, axis=1)
-        acc_s[...] += lax.dot_general(left, right, NT, preferred_element_type=jnp.float32)
-        return count
-
-    count = lax.fori_loop(0, blocks // step, chunk, jnp.zeros((RANGES, LANES), jnp.float32))
+    placed = lax.dot_general(jnp.concatenate(left, axis=1), jnp.concatenate(right, axis=1), NT,
+                             preferred_element_type=jnp.float32)
+
+    def slots(c):
+        rows = placed[c * LANES // 2:(c + 1) * LANES // 2]
+        return jnp.concatenate([rows[:, :RANGES], rows[:, RANGES:]], axis=0)
+
     full = jnp.max(jnp.where(count > CAP, 1.0, 0.0), axis=0, keepdims=True)
     full = jnp.max(full, axis=1, keepdims=True)
 
     slot = iota((LANES, RANGES), 0)
     real = slot < CAP
-    high = acc_s[pl.ds(0, LANES), :]
-    low = acc_s[pl.ds(LANES, LANES), :]
-    sign = jnp.where(real, acc_s[pl.ds(2 * LANES, LANES), :], 0.0)
+    high = slots(0)
+    low = slots(1)
+    sign = jnp.where(real, slots(2), 0.0)
     pos = jnp.maximum(sign, 0.0)
     neg = jnp.maximum(-sign, 0.0)
     p0 = iota((RANGES, RANGES), 0)
@@ -327,8 +335,7 @@
         out_shape=near(4 * RANGES, LANES),
         in_specs=[smem(), vmem(), vmem(), vmem()],
         out_specs=vmem(),
-        scratch_shapes=[pltpu.VMEM((blocks, LANES), jnp.float32)] * 4
-        + [pltpu.VMEM((48, 3 * LANES, LANES), jnp.bfloat16), pltpu.VMEM((3 * LANES, LANES), jnp.float32)],
+        scratch_shapes=[pltpu.VMEM((blocks, LANES), jnp.float32)] * 4,
         name="route",
     )(group_weight, bucket.reshape(blocks, LANES), label.reshape(blocks, LANES), group.reshape(blocks, LANES))
     received = lax.all_to_all(message.reshape(RANGES, 4, LANES), AXES, 0, 0, tiled=True)

time: 50 us -> 49.5 us (0.990)
  Pallas kernels: 6.79 us -> 6.23 us
    pallas_call x1, Pallas kernels: 3.56 us -> 3 us  [on_device(): pl.pallas_call(route_kernel, out_shape=near(4 * RANGES, LANES), in_specs=...]
where the time goes in v4:
time: 49.5 us; the launch traced here: 49.2 us
  blocking collectives  37.8 us (76%)
  Pallas kernels  6.23 us (13%)
  starting transfers between devices  3.37 us (7%)
  loops' own time  0.92 us (2%)
  between operations  0.91 us (2%)
    all_to_all x1, blocking collectives, on_device(): lax.all_to_all(message.reshape(RANGES, 4, LANES), AXES, 0, 0, tiled=True)  22.2 us
    all_to_all x1, blocking collectives, on_device(): parts = lax.all_to_all(parts, AXES, 0, 0, tiled=True)  15.6 us
    ppermute x3, starting transfers between devices, on_device(): lax.ppermute(curves, 'grp', [(i, (i + k) % 4) for i in range(4)])  3.37 us
    pallas_call x1, Pallas kernels, on_device(): pl.pallas_call(route_kernel, out_shape=near(4 * RANGES, LANES), in_specs=...  3 us
    pallas_call x1, Pallas kernels, on_device(): pl.pallas_call(curve_kernel, out_shape=(near(2, ROWS, LANES), near(RANGES...  1.78 us
  transfers between devices with their start and end apart: 3, of which 0 were waited for; matrix products, arithmetic and copies ran while one was open for 0% of the time, Pallas kernels for 1%

profile of v4, /device:TPU:1, one launch (start us, length us, event | category | flops | bytes accessed | tf_op | source)
XLA Modules:
  0.0 49.2 jit_solution(1687749574406420806)
XLA Ops:
  0.6 0.0 copy-start
  0.6 0.0 copy-start.1
  0.7 0.0 copy-start.2
  0.7 0.0 copy-start.3
  0.7 3.0 %route.1 = f32[512,128]{1,0:T(8,128)S(1)} custom-call(f32[16]{0:T(128)} %weights_ref.1, s32[48,128]{1,0:T(8,128)} %bitcast.77, s32[48,128]{1,0:T(8,128)} %bitcast.78, s32[48,128]{1,0:T(8,128)} %bitcast.79), custom_call_target="tpu_custom_call" | custom-call | tf_op jit(solution)/shard_map/route/pallas_call | solution.py:333
  3.7 22.2 %all_to_all.23 = f32[128,4,128]{2,1,0:T(4,128)S(1)} all-to-all(f32[128,4,128]{2,1,0:T(4,128)S(1)} %bitcast.73), channel_id=1, replica_groups=mesh['grp'=4,'shard'=32] {'grp','shard'}, dimensions={0} | all-to-all | bytes 524288 | tf_op jit(solution)/shard_map/all_to_all | solution.py:341
  25.9 1.8 %curve.1 = (f32[2,64,128]{2,1,0:T(8,128)S(1)}, f32[128,1,128]{2,1,0:T(1,128)S(1)}) custom-call(f32[512,128]{1,0:T(8,128)S(1)} %bitcast.72), custom_call_target="tpu_custom_call" | custom-call | tf_op jit(solution)/shard_map/curve/pallas_call | solution.py:342
  27.6 0.3 collective-permute-start
  28.0 1.7 %collective-permute-start.1 = (f32[2,64,128]{2,1,0:T(8,128)S(1)}, f32[2,64,128]{2,1,0:T(8,128)S(1)}, u32[]{:S(2)}, u32[]{:S(2)}) collective-permute-start(f32[2,64,128]{2,1,0:T(8,128)S(1)} %get-tuple-element.138.own_ref), channel_id=1, source_target_pairs={{0,64},{32,96},{64,0},{96,32},{1,65},{33,97},{65,1},{97,33},{2,66}... | collective-permute-start | bytes 196616 | tf_op jit(solution)/shard_map/ppermute | solution.py:350
  29.6 1.4 %collective-permute-start.2 = (f32[2,64,128]{2,1,0:T(8,128)S(1)}, f32[2,64,128]{2,1,0:T(8,128)S(1)}, u32[]{:S(2)}, u32[]{:S(2)}) collective-permute-start(f32[2,64,128]{2,1,0:T(8,128)S(1)} %get-tuple-element.138.own_ref), channel_id=1, source_target_pairs={{0,96},{32,0},{64,32},{96,64},{1,97},{33,1},{65,33},{97,65},{2,98}... | collective-permute-start | bytes 196616 | tf_op jit(solution)/shard_map/ppermute | solution.py:350
  31.0 15.6 %all_to_all.24.part_ref = f32[128,1,128]{2,1,0:T(1,128)S(1)} all-to-all(f32[128,1,128]{2,1,0:T(1,128)S(1)} %get-tuple-element.136), channel_id=1, replica_groups=mesh['grp'=4,'shard'=32] {'grp','shard'}, dimensions={0} | all-to-all | bytes 131072 | tf_op jit(solution)/shard_map/all_to_all | solution.py:349
  46.6 0.7 %area.1 = (f32[1]{0:T(128)}, f32[1]{0:T(128)}, f32[1]{0:T(128)}) custom-call(f32[128,1,128]{2,1,0:T(1,128)S(1)} %all_to_all.24.part_ref), custom_call_target="tpu_custom_call" | custom-call | tf_op jit(solution)/shard_map/area/pallas_call | solution.py:358
  47.4 0.0 collective-permute-done.one_ref
  47.4 0.0 collective-permute-done.1.two_ref
  47.4 0.0 collective-permute-done.2.three_ref
  47.4 0.7 %join.1 = (f32[4,64,128]{2,1,0:T(8,128)}, f32[4,64,128]{2,1,0:T(8,128)}) custom-call(f32[2,64,128]{2,1,0:T(8,128)S(1)} %get-tuple-element.138.own_ref, f32[2,64,128]{2,1,0:T(8,128)S(1)} %collective-permute-done.one_ref, f32[2,64,128]{2,1,0:T(8,128)S(1)} %collective-permute-done.1.two_ref, f32[2,64,128]{2,1,0:T(8,128)S(1)} %collective-permute-done.2.three_ref), custom_call_target="tpu_custom_call" | custom-call | tf_op jit(solution)/shard_map/join/pallas_call | solution.py:351
  48.1 0.0 copy-done
  48.1 0.0 copy-done.1
  48.1 0.0 copy-done.2
  48.1 0.0 copy-done.3
  48.1 0.9 %while.26 = (f32[]{:T(128)}, f32[32768]{0:T(1024)}, f32[32768]{0:T(1024)}, f32[]{:T(128)}, f32[]{:T(128)}, /*index=5*/s32[6144]{0:T(1024)S(1)}, s32[6144]{0:T(1024)S(1)}, f32[16]{0:T(128)S(1)}, s32[6144]{0:T(1024)S(1)}) while((f32[]{:T(128)}, f32[32768]{0:T(1024)}, f32[32768]{0:T(1024)}, f32[]{:T(128)}, f32[]{:T(128)}, /*index=5*/s32[6144]{0:T(1024)S(1)}, ...), condition=%region_12.13_spmd, body=%region_0.12_spmd | while | flops 349572256 | bytes 22732732 | solution.py:370
Async XLA Ops:
  0.6 47.5 %copy-start = (s32[6144]{0:T(1024)S(1)}, s32[6144]{0:T(1024)}, u32[]{:S(2)}) copy-start(s32[6144]{0:T(1024)} %param.8) | copy-start | bytes 73732
  0.6 47.5 %copy-start.1 = (s32[6144]{0:T(1024)S(1)}, s32[6144]{0:T(1024)}, u32[]{:S(2)}) copy-start(s32[6144]{0:T(1024)} %param.9) | copy-start | bytes 73732
  0.7 47.5 %copy-start.2 = (s32[6144]{0:T(1024)S(1)}, s32[6144]{0:T(1024)}, u32[]{:S(2)}) copy-start(s32[6144]{0:T(1024)} %param.10) | copy-start | bytes 73732
  0.7 47.5 %copy-start.3 = (f32[16]{0:T(128)S(1)}, f32[16]{0:T(128)}, u32[]{:S(2)}) copy-start(f32[16]{0:T(128)} %weights_ref.1) | copy-start | bytes 196
  27.6 19.7 %collective-permute-start = (f32[2,64,128]{2,1,0:T(8,128)S(1)}, f32[2,64,128]{2,1,0:T(8,128)S(1)}, u32[]{:S(2)}, u32[]{:S(2)}) collective-permute-start(f32[2,64,128]{2,1,0:T(8,128)S(1)} %get-tuple-element.138.own_ref), channel_id=1, source_target_pairs={{0,32},{32,64},{64,96},{96,0},{1,33},{33,65},{65,97},{97,1},{2,34}... | collective-permute-start | bytes 196616 | tf_op jit(solution)/shard_map/ppermute | solution.py:350
  28.0 19.4 %collective-permute-start.1 = (f32[2,64,128]{2,1,0:T(8,128)S(1)}, f32[2,64,128]{2,1,0:T(8,128)S(1)}, u32[]{:S(2)}, u32[]{:S(2)}) collective-permute-start(f32[2,64,128]{2,1,0:T(8,128)S(1)} %get-tuple-element.138.own_ref), channel_id=1, source_target_pairs={{0,64},{32,96},{64,0},{96,32},{1,65},{33,97},{65,1},{97,33},{2,66}... | collective-permute-start | bytes 196616 | tf_op jit(solution)/shard_map/ppermute | solution.py:350
  29.6 17.7 %collective-permute-start.2 = (f32[2,64,128]{2,1,0:T(8,128)S(1)}, f32[2,64,128]{2,1,0:T(8,128)S(1)}, u32[]{:S(2)}, u32[]{:S(2)}) collective-permute-start(f32[2,64,128]{2,1,0:T(8,128)S(1)} %get-tuple-element.138.own_ref), channel_id=1, source_target_pairs={{0,96},{32,0},{64,32},{96,64},{1,97},{33,1},{65,33},{97,65},{2,98}... | collective-permute-start | bytes 196616 | tf_op jit(solution)/shard_map/ppermute | solution.py:350

commit v5 on v4

--- a/solution.py
+++ b/solution.py
@@ -22,33 +22,9 @@
 HIGHEST = lax.Precision.HIGHEST
 
 
-def copy_for_each(x, axis):
-    count = lax.axis_size(axis)
-    return lax.all_to_all(jnp.broadcast_to(x[None], (count, *x.shape)), axis, 0, 0, tiled=True)
-
-
-def over_copies(x, axis):
-    everything = copy_for_each(x, axis)
-    return jnp.sum(everything, axis=0)
-
-
-def laid_out(tiles, dim):
-    dims = list(tiles.shape[1:])
-    dims[dim] *= tiles.shape[0]
-    return jnp.moveaxis(tiles, 0, dim).reshape(dims)
-
-
-def collect(x, axis, dim):
-    tiles = copy_for_each(x, axis)
-    return laid_out(tiles, dim)
-
-
-def in_one(arrays, axis):
-    ends = [0]
-    for a in arrays:
-        ends.append(ends[-1] + a.size)
-    so_far = over_copies(jnp.concatenate([a.ravel() for a in arrays]), axis)
-    return tuple((so_far[b:e].reshape(a.shape) for a, b, e in zip(arrays, ends, ends[1:])))
+def over_grp(x):
+    every = lax.all_gather(x.reshape(x.size), "grp", axis=0, tiled=True)
+    return jnp.sum(every.reshape(lax.axis_size("grp"), *x.shape), axis=0)
 
 
 def histogram(bucket, label, group, group_weight, start, count):
@@ -96,14 +72,14 @@
     clicks = lax.all_gather(label, "shard", axis=0, tiled=True)
     groups = lax.all_gather(group, "shard", axis=0, tiled=True)
     owned = histogram(ids, clicks, groups, group_weight, first_row, own_rows)
-    owned = over_copies(owned, "grp")
+    owned = jnp.concatenate([over_grp(owned[:own_rows // 2]), over_grp(owned[own_rows // 2:])], axis=0)
     upper = (jnp.arange(LO)[:, None] >= jnp.arange(LO)[None, :]).astype(jnp.float32)
     row_suffix = jnp.dot(owned.reshape(own_rows * 2, LO), upper, precision=HIGHEST)
     row_totals = jnp.sum(owned, axis=2)
     strict = (jnp.arange(own_rows)[None, :] > jnp.arange(own_rows)[:, None]).astype(jnp.float32)
     after = jnp.dot(strict, row_totals, precision=HIGHEST)
     range_total = jnp.sum(row_totals, axis=0)
-    every = collect(range_total[None, :], "shard", 0)
+    every = lax.all_gather(range_total, "shard")
     later = jnp.arange(shards) > lax.axis_index("shard")
     higher = jnp.sum(jnp.where(later[:, None], every, 0.0), axis=0)
     overall = jnp.sum(every, axis=0)
@@ -116,7 +92,7 @@
     precision = true_pos / jnp.maximum(true_pos + false_pos, 1.0)
     roc_part = jnp.sum(neg_hist * (2.0 * true_pos - pos_hist))
     prc_part = jnp.sum(pos_hist * precision)
-    roc_sum, prc_sum = in_one((roc_part, prc_part), "shard")
+    roc_sum, prc_sum = lax.psum((roc_part, prc_part), "shard")
     auroc = roc_sum / (2.0 * overall[0] * overall[1])
     auprc = prc_sum / overall[0]
     return (tpr_curve, precision.reshape(own_rows * LO), auroc, auprc)
@@ -232,7 +208,7 @@
     return first, second, rest.astype(jnp.bfloat16)
 
 
-def curve_kernel(in_ref, curve_ref, part_ref):
+def curve_kernel(in_ref, curve_ref, part_ref, fix_ref, flag_ref):
     step = 128
     none = jnp.zeros((16, LANES), jnp.bfloat16)
     unit = jnp.ones((16, LANES), jnp.bfloat16)
@@ -290,6 +266,8 @@
     prc = jnp.sum(prc, axis=1, keepdims=True) / total_pos
     lane = iota((RANGES, 1, LANES), 2)
     part_ref[...] = jnp.where(lane == 0, roc[None], jnp.where(lane == 1, prc[None], flag[None]))
+    fix_ref[...] = jnp.zeros((8, LANES), jnp.float32)
+    flag_ref[0] = jnp.max(flag)
 
 
 def join_kernel(own_ref, one_ref, two_ref, three_ref, tpr_ref, precision_ref):
@@ -300,12 +278,20 @@
         precision_ref[source] = ref[1]
 
 
-def area_kernel(part_ref, roc_ref, prc_ref, flag_ref):
+def area_kernel(part_ref, fix_ref, roc_ref, prc_ref, fix_s, done):
     sums = jnp.sum(part_ref[...].reshape(RANGES, LANES), axis=0, keepdims=True)
     lane = iota((1, LANES), 1)
     roc_ref[0] = jnp.sum(jnp.where(lane == 0, sums, 0.0))
     prc_ref[0] = jnp.sum(jnp.where(lane == 1, sums, 0.0))
-    flag_ref[0] = jnp.sum(jnp.where(lane == 2, sums, 0.0))
+
+    @pl.when(jnp.sum(jnp.where(lane == 2, sums, 0.0)) > 0.0)
+    def _():
+        copy = pltpu.make_async_copy(fix_ref, fix_s, done)
+        copy.start()
+        copy.wait()
+        fix = fix_s[0:1, :]
+        roc_ref[0] = jnp.sum(jnp.where(lane == 0, fix, 0.0))
+        prc_ref[0] = jnp.sum(jnp.where(lane == 1, fix, 0.0))
 
 
 def vmem():
@@ -339,11 +325,11 @@
         name="route",
     )(group_weight, bucket.reshape(blocks, LANES), label.reshape(blocks, LANES), group.reshape(blocks, LANES))
     received = lax.all_to_all(message.reshape(RANGES, 4, LANES), AXES, 0, 0, tiled=True)
-    curves, parts = pl.pallas_call(
+    curves, parts, fix, flag = pl.pallas_call(
         curve_kernel,
-        out_shape=(near(2, ROWS, LANES), near(RANGES, 1, LANES)),
+        out_shape=(near(2, ROWS, LANES), near(RANGES, 1, LANES), f32(8, LANES), f32(1)),
         in_specs=[vmem()],
-        out_specs=(vmem(), vmem()),
+        out_specs=(vmem(), vmem(), vmem(), smem()),
         name="curve",
     )(at_hand(received.reshape(4 * RANGES, LANES)))
     parts = lax.all_to_all(parts, AXES, 0, 0, tiled=True)
@@ -355,20 +341,26 @@
         out_specs=(vmem(), vmem()),
         name="join",
     )(at_hand(curves), *[at_hand(x) for x in others])
-    roc, prc, flag = pl.pallas_call(
+    size = 4 * ROWS * LANES
+
+    def again(state):
+        nothing = (state[0] < 0.0).astype(jnp.int32)
+        tpr, precision, roc, prc = general(bucket + nothing, label + nothing, group + nothing, group_weight)
+        fix = jnp.where(jnp.arange(LANES)[None, :] == 0, roc, prc)
+        return jnp.zeros((), jnp.float32), jnp.broadcast_to(fix, (8, LANES)), tpr, precision
+
+    _, fix, tpr, precision = lax.while_loop(
+        lambda state: state[0] > 0.0, again,
+        (flag.reshape(()), fix, tpr.reshape(size), precision.reshape(size)))
+    roc, prc = pl.pallas_call(
         area_kernel,
-        out_shape=(f32(1), f32(1), f32(1)),
-        in_specs=[vmem()],
-        out_specs=(smem(), smem(), smem()),
+        out_shape=(f32(1), f32(1)),
+        in_specs=[vmem(), pl.BlockSpec(memory_space=pl.ANY)],
+        out_specs=(smem(), smem()),
+        scratch_shapes=[pltpu.VMEM((8, LANES), jnp.float32), pltpu.SemaphoreType.DMA],
         name="area",
-    )(at_hand(parts))
-    quick = (tpr.reshape(4 * ROWS * LANES), precision.reshape(4 * ROWS * LANES), roc.reshape(()), prc.reshape(()))
-
-    def again(state):
-        return (jnp.zeros((), jnp.float32), *general(bucket, label, group, group_weight))
-
-    state = lax.while_loop(lambda s: s[0] > 0.0, again, (flag.reshape(()), *quick))
-    return state[1:]
+    )(at_hand(parts), fix)
+    return tpr, precision, roc.reshape(()), prc.reshape(())
 
 
 def solution(mesh):

time: 49.5 us -> 48.6 us (0.982)
  blocking collectives: 37.8 us -> 22.2 us
  waiting for transfers between devices: 0.01 us -> 7.87 us
  starting transfers between devices: 3.37 us -> 9.66 us
  Pallas kernels: 6.23 us -> 6.87 us
    all_to_all x1 -> x0, blocking collectives: 15.6 us -> none  [on_device(): parts = lax.all_to_all(parts, AXES, 0, 0, tiled=True)]
    all_to_all x0 -> x1, waiting for transfers between devices: none -> 7.86 us  [on_device(): parts = lax.all_to_all(parts, AXES, 0, 0, tiled=True)]
    all_to_all x0 -> x1, starting transfers between devices: none -> 6.27 us  [on_device(): parts = lax.all_to_all(parts, AXES, 0, 0, tiled=True)]
    pallas_call x1, Pallas kernels: 1.78 us -> 2.41 us  [on_device(): pl.pallas_call(curve_kernel, out_shape=(near(2, ROWS, LANES), near(RANGES...]
  transfers between devices with their start and end apart: 3 -> 4, of which waited for: 0 -> 1; matrix products, arithmetic and copies ran while one was open for 0% -> 0% of each run, Pallas kernels for 1% -> 2%
where the time goes in v5:
time: 48.6 us; the launch traced here: 48.4 us
  blocking collectives  22.2 us (46%)
  starting transfers between devices  9.66 us (20%)
  waiting for transfers between devices  7.87 us (16%)
  Pallas kernels  6.87 us (14%)
  between operations  0.91 us (2%)
  loops' own time  0.87 us (2%)
    all_to_all x1, blocking collectives, on_device(): lax.all_to_all(message.reshape(RANGES, 4, LANES), AXES, 0, 0, tiled=True)  22.2 us
    all_to_all x1, waiting for transfers between devices, on_device(): parts = lax.all_to_all(parts, AXES, 0, 0, tiled=True)  7.86 us
    all_to_all x1, starting transfers between devices, on_device(): parts = lax.all_to_all(parts, AXES, 0, 0, tiled=True)  6.27 us
    ppermute x3, starting transfers between devices, on_device(): lax.ppermute(curves, 'grp', [(i, (i + k) % 4) for i in range(4)])  3.38 us
    pallas_call x1, Pallas kernels, on_device(): pl.pallas_call(route_kernel, out_shape=near(4 * RANGES, LANES), in_specs=...  3 us
    pallas_call x1, Pallas kernels, on_device(): pl.pallas_call(curve_kernel, out_shape=(near(2, ROWS, LANES), near(RANGES...  2.41 us
  transfers between devices with their start and end apart: 4, of which 1 were waited for; matrix products, arithmetic and copies ran while one was open for 0% of the time, Pallas kernels for 2%

profile of v5, /device:TPU:1, one launch (start us, length us, event | category | flops | bytes accessed | tf_op | source)
XLA Modules:
  0.0 48.4 jit_solution(17910034616057559113)
XLA Ops:
  0.6 0.0 copy-start.2
  0.6 0.0 copy-start
  0.7 0.0 copy-start.1
  0.7 0.0 copy-start.3
  0.7 3.0 %route.1 = f32[512,128]{1,0:T(8,128)S(1)} custom-call(f32[16]{0:T(128)} %weights_ref.1, s32[48,128]{1,0:T(8,128)} %bitcast.78, s32[48,128]{1,0:T(8,128)} %bitcast.79, s32[48,128]{1,0:T(8,128)} %bitcast.80), custom_call_target="tpu_custom_call" | custom-call | tf_op jit(solution)/shard_map/route/pallas_call | solution.py:319
  3.7 22.2 %all_to_all.10 = f32[128,4,128]{2,1,0:T(4,128)S(1)} all-to-all(f32[128,4,128]{2,1,0:T(4,128)S(1)} %bitcast.72), channel_id=1, replica_groups=mesh['grp'=4,'shard'=32] {'grp','shard'}, dimensions={0} | all-to-all | bytes 524288 | tf_op jit(solution)/shard_map/all_to_all | solution.py:327
  25.9 2.4 %curve.1 = (f32[2,64,128]{2,1,0:T(8,128)S(1)}, f32[128,1,128]{2,1,0:T(1,128)}, f32[8,128]{1,0:T(8,128)}, f32[1]{0:T(128)}) custom-call(f32[512,128]{1,0:T(8,128)S(1)} %bitcast.71), custom_call_target="tpu_custom_call" | custom-call | tf_op jit(solution)/shard_map/curve/pallas_call | solution.py:328
  28.3 0.3 collective-permute-start
  28.6 1.7 %collective-permute-start.1 = (f32[2,64,128]{2,1,0:T(8,128)S(1)}, f32[2,64,128]{2,1,0:T(8,128)S(1)}, u32[]{:S(2)}, u32[]{:S(2)}) collective-permute-start(f32[2,64,128]{2,1,0:T(8,128)S(1)} %get-tuple-element.135.own_ref), channel_id=1, source_target_pairs={{0,64},{32,96},{64,0},{96,32},{1,65},{33,97},{65,1},{97,33},{2,66}... | collective-permute-start | bytes 196616 | tf_op jit(solution)/shard_map/ppermute | solution.py:336
  30.3 1.4 %collective-permute-start.2 = (f32[2,64,128]{2,1,0:T(8,128)S(1)}, f32[2,64,128]{2,1,0:T(8,128)S(1)}, u32[]{:S(2)}, u32[]{:S(2)}) collective-permute-start(f32[2,64,128]{2,1,0:T(8,128)S(1)} %get-tuple-element.135.own_ref), channel_id=1, source_target_pairs={{0,96},{32,0},{64,32},{96,64},{1,97},{33,1},{65,33},{97,65},{2,98}... | collective-permute-start | bytes 196616 | tf_op jit(solution)/shard_map/ppermute | solution.py:336
  31.7 6.3 %all-to-all-start.1 = ((f32[128,1,128]{2,1,0:T(1,128)}), f32[128,1,128]{2,1,0:T(1,128)S(1)}, u32[]{:S(2)}, u32[]{:S(2)}) async-start(f32[128,1,128]{2,1,0:T(1,128)} %get-tuple-element.140), calls=%async_computation.1 | async-start | bytes 131072 | tf_op jit(solution)/shard_map/all_to_all | solution.py:335
  37.9 0.0 collective-permute-done.one_ref
  37.9 0.0 collective-permute-done.1.two_ref
  38.0 0.0 collective-permute-done.2.three_ref
  38.0 0.7 %join.1 = (f32[4,64,128]{2,1,0:T(8,128)}, f32[4,64,128]{2,1,0:T(8,128)}) custom-call(f32[2,64,128]{2,1,0:T(8,128)S(1)} %get-tuple-element.135.own_ref, f32[2,64,128]{2,1,0:T(8,128)S(1)} %collective-permute-done.one_ref, f32[2,64,128]{2,1,0:T(8,128)S(1)} %collective-permute-done.1.two_ref, f32[2,64,128]{2,1,0:T(8,128)S(1)} %collective-permute-done.2.three_ref), custom_call_target="tpu_custom_call" | custom-call | tf_op jit(solution)/shard_map/join/pallas_call | solution.py:337
  38.7 0.0 copy-done.2
  38.7 0.0 copy-done
  38.7 0.0 copy-done.1
  38.7 0.0 copy-done.3
  38.7 0.9 %while.24 = (f32[]{:T(128)}, f32[8,128]{1,0:T(8,128)}, f32[32768]{0:T(1024)}, f32[32768]{0:T(1024)}, s32[6144]{0:T(1024)S(1)}, /*index=5*/s32[6144]{0:T(1024)S(1)}, f32[16]{0:T(128)S(1)}, s32[6144]{0:T(1024)S(1)}) while((f32[]{:T(128)}, f32[8,128]{1,0:T(8,128)}, f32[32768]{0:T(1024)}, f32[32768]{0:T(1024)}, s32[6144]{0:T(1024)S(1)}, ...), condition=%region_15.16_spmd, body=%region_0.15_spmd | while | flops 349394336 | bytes 22558096 | solution.py:352
  39.6 7.9 %all-to-all-done.1.part_ref = f32[128,1,128]{2,1,0:T(1,128)S(1)} async-done(((f32[128,1,128]{2,1,0:T(1,128)}), f32[128,1,128]{2,1,0:T(1,128)S(1)}, u32[]{:S(2)}, u32[]{:S(2)}) %all-to-all-start.1) | async-done | bytes 65568 | tf_op jit(solution)/shard_map/all_to_all | solution.py:335
  47.5 0.7 %area.1 = (f32[1]{0:T(128)}, f32[1]{0:T(128)}) custom-call(f32[128,1,128]{2,1,0:T(1,128)S(1)} %all-to-all-done.1.part_ref, f32[8,128]{1,0:T(8,128)} %get-tuple-element.141.fix_ref), custom_call_target="tpu_custom_call" | custom-call | tf_op jit(solution)/shard_map/area/pallas_call | solution.py:355
Async XLA Ops:
  0.6 38.1 %copy-start.2 = (s32[6144]{0:T(1024)S(1)}, s32[6144]{0:T(1024)}, u32[]{:S(2)}) copy-start(s32[6144]{0:T(1024)} %param.10) | copy-start | bytes 73732
  0.6 38.1 %copy-start = (s32[6144]{0:T(1024)S(1)}, s32[6144]{0:T(1024)}, u32[]{:S(2)}) copy-start(s32[6144]{0:T(1024)} %param.8) | copy-start | bytes 73732
  0.7 38.1 %copy-start.1 = (s32[6144]{0:T(1024)S(1)}, s32[6144]{0:T(1024)}, u32[]{:S(2)}) copy-start(s32[6144]{0:T(1024)} %param.9) | copy-start | bytes 73732
  0.7 38.0 %copy-start.3 = (f32[16]{0:T(128)S(1)}, f32[16]{0:T(128)}, u32[]{:S(2)}) copy-start(f32[16]{0:T(128)} %weights_ref.1) | copy-start | bytes 196
  28.3 9.7 %collective-permute-start = (f32[2,64,128]{2,1,0:T(8,128)S(1)}, f32[2,64,128]{2,1,0:T(8,128)S(1)}, u32[]{:S(2)}, u32[]{:S(2)}) collective-permute-start(f32[2,64,128]{2,1,0:T(8,128)S(1)} %get-tuple-element.135.own_ref), channel_id=1, source_target_pairs={{0,32},{32,64},{64,96},{96,0},{1,33},{33,65},{65,97},{97,1},{2,34}... | collective-permute-start | bytes 196616 | tf_op jit(solution)/shard_map/ppermute | solution.py:336
  28.6 9.3 %collective-permute-start.1 = (f32[2,64,128]{2,1,0:T(8,128)S(1)}, f32[2,64,128]{2,1,0:T(8,128)S(1)}, u32[]{:S(2)}, u32[]{:S(2)}) collective-permute-start(f32[2,64,128]{2,1,0:T(8,128)S(1)} %get-tuple-element.135.own_ref), channel_id=1, source_target_pairs={{0,64},{32,96},{64,0},{96,32},{1,65},{33,97},{65,1},{97,33},{2,66}... | collective-permute-start | bytes 196616 | tf_op jit(solution)/shard_map/ppermute | solution.py:336
  30.3 7.7 %collective-permute-start.2 = (f32[2,64,128]{2,1,0:T(8,128)S(1)}, f32[2,64,128]{2,1,0:T(8,128)S(1)}, u32[]{:S(2)}, u32[]{:S(2)}) collective-permute-start(f32[2,64,128]{2,1,0:T(8,128)S(1)} %get-tuple-element.135.own_ref), channel_id=1, source_target_pairs={{0,96},{32,0},{64,32},{96,64},{1,97},{33,1},{65,33},{97,65},{2,98}... | collective-permute-start | bytes 196616 | tf_op jit(solution)/shard_map/ppermute | solution.py:336
  31.7 15.8 %all-to-all-start.1 = ((f32[128,1,128]{2,1,0:T(1,128)}), f32[128,1,128]{2,1,0:T(1,128)S(1)}, u32[]{:S(2)}, u32[]{:S(2)}) async-start(f32[128,1,128]{2,1,0:T(1,128)} %get-tuple-element.140), calls=%async_computation.1 | async-start | bytes 131072 | tf_op jit(solution)/shard_map/all_to_all | solution.py:335

commit v6 on v5

--- a/solution.py
+++ b/solution.py
@@ -191,13 +191,12 @@
     above = (r0 > r1).astype(jnp.bfloat16)
     both = jnp.concatenate([pos, neg], axis=0).astype(jnp.bfloat16)
     later = lax.dot_general(both, above, NN, preferred_element_type=jnp.float32)
-    for c, own in ((2, pos), (3, neg)):
-        higher = jnp.sum(later[(c - 2) * LANES:(c - 1) * LANES], axis=0, keepdims=True)
+    for c, own in ((1, pos), (2, neg)):
+        higher = jnp.sum(later[(c - 1) * LANES:c * LANES], axis=0, keepdims=True)
         total = jnp.sum(jnp.sum(own, axis=0, keepdims=True), axis=1, keepdims=True)
         sent = jnp.where(real, own, jnp.where(slot == CAP, higher, total))
-        out_ref[pl.ds(c, RANGES, stride=4), :] = sent.T
-    out_ref[pl.ds(0, RANGES, stride=4), :] = jnp.where(real, high, full).T
-    out_ref[pl.ds(1, RANGES, stride=4), :] = low.T
+        out_ref[pl.ds(c, RANGES, stride=3), :] = sent.T
+    out_ref[pl.ds(0, RANGES, stride=3), :] = jnp.where(real, LANES * high + low, full).T
 
 
 def in_three(x):
@@ -209,40 +208,35 @@
 
 
 def curve_kernel(in_ref, curve_ref, part_ref, fix_ref, flag_ref):
-    step = 128
     none = jnp.zeros((16, LANES), jnp.bfloat16)
     unit = jnp.ones((16, LANES), jnp.bfloat16)
     first = iota((16, LANES), 0).astype(jnp.float32).astype(jnp.bfloat16)
     real = iota((16, LANES), 1) < CAP
-
-    def chunk(i, carry):
-        hist, sums = carry
-        left = []
-        right = []
-        for u in range(step):
-            at = (i * step + u) * 4
-            high = bf16_rows(in_ref[pl.ds(at, 1), :])
-            low = bf16_rows(in_ref[pl.ds(at + 1, 1), :])
-            pos = jnp.where(real, jnp.broadcast_to(in_ref[pl.ds(at + 2, 1), :], (16, LANES)), 0.0).astype(jnp.bfloat16)
-            neg = jnp.where(real, jnp.broadcast_to(in_ref[pl.ds(at + 3, 1), :], (16, LANES)), 0.0).astype(jnp.bfloat16)
-            same = [first + jnp.bfloat16(16 * k) == high for k in range(4)]
-            left.append(jnp.concatenate(
-                [jnp.where(m, pos, none) for m in same] + [jnp.where(m, neg, none) for m in same], axis=0))
-            right.append(jnp.concatenate(one_hot(low, 8, unit, none), axis=0))
-        hist = hist + lax.dot_general(jnp.concatenate(left, axis=1), jnp.concatenate(right, axis=1), NT,
-                                      preferred_element_type=jnp.float32)
-        for u in range(step // 2):
-            sums = sums + in_ref[pl.ds((i * step + 2 * u) * 4, 8), :]
-        return hist, sums
-
-    start = (jnp.zeros((2 * ROWS, LANES), jnp.float32), jnp.zeros((8, LANES), jnp.float32))
-    hist, sums = lax.fori_loop(0, RANGES // step, chunk, start)
-    sums = sums[0:4] + sums[4:8]
-    flag = sums[0:1, CAP:CAP + 1]
-    higher_pos = sums[2:3, CAP:CAP + 1]
-    total_pos = sums[2:3, CAP + 1:CAP + 2]
-    higher_neg = sums[3:4, CAP:CAP + 1]
-    total_neg = sums[3:4, CAP + 1:CAP + 2]
+    left = []
+    right = []
+    for q in range(RANGES):
+        place = in_ref[pl.ds(3 * q, 1), :]
+        high = jnp.floor(place * (1.0 / LANES))
+        low = bf16_rows(place - LANES * high)
+        high = bf16_rows(high)
+        pos = jnp.where(real, jnp.broadcast_to(in_ref[pl.ds(3 * q + 1, 1), :], (16, LANES)), 0.0).astype(jnp.bfloat16)
+        neg = jnp.where(real, jnp.broadcast_to(in_ref[pl.ds(3 * q + 2, 1), :], (16, LANES)), 0.0).astype(jnp.bfloat16)
+        same = [first + jnp.bfloat16(16 * k) == high for k in range(4)]
+        left.append(jnp.concatenate(
+            [jnp.where(m, pos, none) for m in same] + [jnp.where(m, neg, none) for m in same], axis=0))
+        right.append(jnp.concatenate(one_hot(low, 8, unit, none), axis=0))
+    hist = lax.dot_general(jnp.concatenate(left, axis=1), jnp.concatenate(right, axis=1), NT,
+                           preferred_element_type=jnp.float32)
+    sums = in_ref[pl.ds(0, 24), :]
+    for q in range(24, 3 * RANGES, 24):
+        sums = sums + in_ref[pl.ds(q, 24), :]
+    kind = iota((24, LANES), 0) % 3
+    sums = [jnp.sum(jnp.where(kind == c, sums, 0.0), axis=0, keepdims=True) for c in range(3)]
+    flag = sums[0][:, CAP:CAP + 1]
+    higher_pos = sums[1][:, CAP:CAP + 1]
+    total_pos = sums[1][:, CAP + 1:CAP + 2]
+    higher_neg = sums[2][:, CAP:CAP + 1]
+    total_neg = sums[2][:, CAP + 1:CAP + 2]
     upper = (iota((LANES, LANES), 0) >= iota((LANES, LANES), 1)).astype(jnp.bfloat16)
     row = iota((2 * ROWS, 2 * ROWS), 0)
     col = iota((2 * ROWS, 2 * ROWS), 1)
@@ -318,20 +312,20 @@
     blocks = bucket.shape[0] // LANES
     message = pl.pallas_call(
         route_kernel,
-        out_shape=near(4 * RANGES, LANES),
+        out_shape=near(3 * RANGES, LANES),
         in_specs=[smem(), vmem(), vmem(), vmem()],
         out_specs=vmem(),
         scratch_shapes=[pltpu.VMEM((blocks, LANES), jnp.float32)] * 4,
         name="route",
     )(group_weight, bucket.reshape(blocks, LANES), label.reshape(blocks, LANES), group.reshape(blocks, LANES))
-    received = lax.all_to_all(message.reshape(RANGES, 4, LANES), AXES, 0, 0, tiled=True)
+    received = lax.all_to_all(message.reshape(RANGES, 1, 3 * LANES), AXES, 0, 0, tiled=True)
     curves, parts, fix, flag = pl.pallas_call(
         curve_kernel,
         out_shape=(near(2, ROWS, LANES), near(RANGES, 1, LANES), f32(8, LANES), f32(1)),
         in_specs=[vmem()],
         out_specs=(vmem(), vmem(), vmem(), smem()),
         name="curve",
-    )(at_hand(received.reshape(4 * RANGES, LANES)))
+    )(at_hand(received.reshape(3 * RANGES, LANES)))
     parts = lax.all_to_all(parts, AXES, 0, 0, tiled=True)
     others = [lax.ppermute(curves, "grp", [(i, (i + k) % 4) for i in range(4)]) for k in (1, 2, 3)]
     tpr, precision = pl.pallas_call(

time: 48.6 us -> 47.9 us (0.986)
  blocking collectives: 22.2 us -> 21.7 us
where the time goes in v6:
time: 47.9 us; the launch traced here: 47.7 us
  blocking collectives  21.7 us (45%)
  starting transfers between devices  9.47 us (20%)
  waiting for transfers between devices  7.87 us (16%)
  Pallas kernels  6.84 us (14%)
  between operations  0.91 us (2%)
  loops' own time  0.87 us (2%)
    all_to_all x1, blocking collectives, on_device(): lax.all_to_all(message.reshape(RANGES, 1, 3 * LANES), AXES, 0, 0, tiled=T...  21.7 us
    all_to_all x1, waiting for transfers between devices, on_device(): parts = lax.all_to_all(parts, AXES, 0, 0, tiled=True)  7.86 us
    all_to_all x1, starting transfers between devices, on_device(): parts = lax.all_to_all(parts, AXES, 0, 0, tiled=True)  6.18 us
    ppermute x3, starting transfers between devices, on_device(): lax.ppermute(curves, 'grp', [(i, (i + k) % 4) for i in range(4)])  3.29 us
    pallas_call x1, Pallas kernels, on_device(): pl.pallas_call(route_kernel, out_shape=near(3 * RANGES, LANES), in_specs=...  2.98 us
    pallas_call x1, Pallas kernels, on_device(): pl.pallas_call(curve_kernel, out_shape=(near(2, ROWS, LANES), near(RANGES...  2.4 us
  transfers between devices with their start and end apart: 4, of which 1 were waited for; matrix products, arithmetic and copies ran while one was open for 0% of the time, Pallas kernels for 2%

profile of v6, /device:TPU:1, one launch (start us, length us, event | category | flops | bytes accessed | tf_op | source)
XLA Modules:
  0.0 47.7 jit_solution(4406442745204267490)
XLA Ops:
  0.6 0.0 copy-start.2
  0.6 0.0 copy-start
  0.7 0.0 copy-start.1
  0.7 0.0 copy-start.3
  0.7 3.0 %route.1 = f32[384,128]{1,0:T(8,128)S(1)} custom-call(f32[16]{0:T(128)} %weights_ref.1, s32[48,128]{1,0:T(8,128)} %bitcast.78, s32[48,128]{1,0:T(8,128)} %bitcast.79, s32[48,128]{1,0:T(8,128)} %bitcast.80), custom_call_target="tpu_custom_call" | custom-call | tf_op jit(solution)/shard_map/route/pallas_call | solution.py:313
  3.7 21.7 %all_to_all.10 = f32[128,1,384]{2,1,0:T(1,128)S(1)} all-to-all(f32[128,1,384]{2,1,0:T(1,128)S(1)} %bitcast.72), channel_id=1, replica_groups=mesh['grp'=4,'shard'=32] {'grp','shard'}, dimensions={0} | all-to-all | bytes 393216 | tf_op jit(solution)/shard_map/all_to_all | solution.py:321
  25.4 2.4 %curve.1 = (f32[2,64,128]{2,1,0:T(8,128)S(1)}, f32[128,1,128]{2,1,0:T(1,128)}, f32[8,128]{1,0:T(8,128)}, f32[1]{0:T(128)}) custom-call(f32[384,128]{1,0:T(8,128)S(1)} %bitcast.71), custom_call_target="tpu_custom_call" | custom-call | tf_op jit(solution)/shard_map/curve/pallas_call | solution.py:322
  27.8 0.4 collective-permute-start
  28.2 1.7 %collective-permute-start.1 = (f32[2,64,128]{2,1,0:T(8,128)S(1)}, f32[2,64,128]{2,1,0:T(8,128)S(1)}, u32[]{:S(2)}, u32[]{:S(2)}) collective-permute-start(f32[2,64,128]{2,1,0:T(8,128)S(1)} %get-tuple-element.135.own_ref), channel_id=1, source_target_pairs={{0,64},{32,96},{64,0},{96,32},{1,65},{33,97},{65,1},{97,33},{2,66}... | collective-permute-start | bytes 196616 | tf_op jit(solution)/shard_map/ppermute | solution.py:330
  29.8 1.2 %collective-permute-start.2 = (f32[2,64,128]{2,1,0:T(8,128)S(1)}, f32[2,64,128]{2,1,0:T(8,128)S(1)}, u32[]{:S(2)}, u32[]{:S(2)}) collective-permute-start(f32[2,64,128]{2,1,0:T(8,128)S(1)} %get-tuple-element.135.own_ref), channel_id=1, source_target_pairs={{0,96},{32,0},{64,32},{96,64},{1,97},{33,1},{65,33},{97,65},{2,98}... | collective-permute-start | bytes 196616 | tf_op jit(solution)/shard_map/ppermute | solution.py:330
  31.1 6.2 %all-to-all-start.1 = ((f32[128,1,128]{2,1,0:T(1,128)}), f32[128,1,128]{2,1,0:T(1,128)S(1)}, u32[]{:S(2)}, u32[]{:S(2)}) async-start(f32[128,1,128]{2,1,0:T(1,128)} %get-tuple-element.140), calls=%async_computation.1 | async-start | bytes 131072 | tf_op jit(solution)/shard_map/all_to_all | solution.py:329
  37.3 0.0 collective-permute-done.one_ref
  37.3 0.0 collective-permute-done.1.two_ref
  37.3 0.0 collective-permute-done.2.three_ref
  37.3 0.7 %join.1 = (f32[4,64,128]{2,1,0:T(8,128)}, f32[4,64,128]{2,1,0:T(8,128)}) custom-call(f32[2,64,128]{2,1,0:T(8,128)S(1)} %get-tuple-element.135.own_ref, f32[2,64,128]{2,1,0:T(8,128)S(1)} %collective-permute-done.one_ref, f32[2,64,128]{2,1,0:T(8,128)S(1)} %collective-permute-done.1.two_ref, f32[2,64,128]{2,1,0:T(8,128)S(1)} %collective-permute-done.2.three_ref), custom_call_target="tpu_custom_call" | custom-call | tf_op jit(solution)/shard_map/join/pallas_call | solution.py:331
  38.0 0.0 copy-done.2
  38.0 0.0 copy-done
  38.0 0.0 copy-done.1
  38.0 0.0 copy-done.3
  38.0 0.9 %while.24 = (f32[]{:T(128)}, f32[8,128]{1,0:T(8,128)}, f32[32768]{0:T(1024)}, f32[32768]{0:T(1024)}, s32[6144]{0:T(1024)S(1)}, /*index=5*/s32[6144]{0:T(1024)S(1)}, f32[16]{0:T(128)S(1)}, s32[6144]{0:T(1024)S(1)}) while((f32[]{:T(128)}, f32[8,128]{1,0:T(8,128)}, f32[32768]{0:T(1024)}, f32[32768]{0:T(1024)}, s32[6144]{0:T(1024)S(1)}, ...), condition=%region_15.16_spmd, body=%region_0.15_spmd | while | flops 349394336 | bytes 22558096 | solution.py:346
  38.9 7.9 %all-to-all-done.1.part_ref = f32[128,1,128]{2,1,0:T(1,128)S(1)} async-done(((f32[128,1,128]{2,1,0:T(1,128)}), f32[128,1,128]{2,1,0:T(1,128)S(1)}, u32[]{:S(2)}, u32[]{:S(2)}) %all-to-all-start.1) | async-done | bytes 65568 | tf_op jit(solution)/shard_map/all_to_all | solution.py:329
  46.8 0.7 %area.1 = (f32[1]{0:T(128)}, f32[1]{0:T(128)}) custom-call(f32[128,1,128]{2,1,0:T(1,128)S(1)} %all-to-all-done.1.part_ref, f32[8,128]{1,0:T(8,128)} %get-tuple-element.141.fix_ref), custom_call_target="tpu_custom_call" | custom-call | tf_op jit(solution)/shard_map/area/pallas_call | solution.py:349
Async XLA Ops:
  0.6 37.4 %copy-start.2 = (s32[6144]{0:T(1024)S(1)}, s32[6144]{0:T(1024)}, u32[]{:S(2)}) copy-start(s32[6144]{0:T(1024)} %param.10) | copy-start | bytes 73732
  0.6 37.4 %copy-start = (s32[6144]{0:T(1024)S(1)}, s32[6144]{0:T(1024)}, u32[]{:S(2)}) copy-start(s32[6144]{0:T(1024)} %param.8) | copy-start | bytes 73732
  0.7 37.4 %copy-start.1 = (s32[6144]{0:T(1024)S(1)}, s32[6144]{0:T(1024)}, u32[]{:S(2)}) copy-start(s32[6144]{0:T(1024)} %param.9) | copy-start | bytes 73732
  0.7 37.4 %copy-start.3 = (f32[16]{0:T(128)S(1)}, f32[16]{0:T(128)}, u32[]{:S(2)}) copy-start(f32[16]{0:T(128)} %weights_ref.1) | copy-start | bytes 196
  27.8 9.5 %collective-permute-start = (f32[2,64,128]{2,1,0:T(8,128)S(1)}, f32[2,64,128]{2,1,0:T(8,128)S(1)}, u32[]{:S(2)}, u32[]{:S(2)}) collective-permute-start(f32[2,64,128]{2,1,0:T(8,128)S(1)} %get-tuple-element.135.own_ref), channel_id=1, source_target_pairs={{0,32},{32,64},{64,96},{96,0},{1,33},{33,65},{65,97},{97,1},{2,34}... | collective-permute-start | bytes 196616 | tf_op jit(solution)/shard_map/ppermute | solution.py:330
  28.2 9.1 %collective-permute-start.1 = (f32[2,64,128]{2,1,0:T(8,128)S(1)}, f32[2,64,128]{2,1,0:T(8,128)S(1)}, u32[]{:S(2)}, u32[]{:S(2)}) collective-permute-start(f32[2,64,128]{2,1,0:T(8,128)S(1)} %get-tuple-element.135.own_ref), channel_id=1, source_target_pairs={{0,64},{32,96},{64,0},{96,32},{1,65},{33,97},{65,1},{97,33},{2,66}... | collective-permute-start | bytes 196616 | tf_op jit(solution)/shard_map/ppermute | solution.py:330
  29.8 7.4 %collective-permute-start.2 = (f32[2,64,128]{2,1,0:T(8,128)S(1)}, f32[2,64,128]{2,1,0:T(8,128)S(1)}, u32[]{:S(2)}, u32[]{:S(2)}) collective-permute-start(f32[2,64,128]{2,1,0:T(8,128)S(1)} %get-tuple-element.135.own_ref), channel_id=1, source_target_pairs={{0,96},{32,0},{64,32},{96,64},{1,97},{33,1},{65,33},{97,65},{2,98}... | collective-permute-start | bytes 196616 | tf_op jit(solution)/shard_map/ppermute | solution.py:330
  31.1 15.7 %all-to-all-start.1 = ((f32[128,1,128]{2,1,0:T(1,128)}), f32[128,1,128]{2,1,0:T(1,128)S(1)}, u32[]{:S(2)}, u32[]{:S(2)}) async-start(f32[128,1,128]{2,1,0:T(1,128)} %get-tuple-element.140), calls=%async_computation.1 | async-start | bytes 131072 | tf_op jit(solution)/shard_map/all_to_all | solution.py:329

commit v7 on v6

--- a/solution.py
+++ b/solution.py
@@ -10,6 +10,7 @@
 BLOCK = 1024
 HI = 4096
 BATCH = 6
+CHUNK = 12
 
 AXES = ("grp", "shard")
 LANES = 128
@@ -148,11 +149,14 @@
         seen_all = lax.dot_general(jnp.concatenate(batch, axis=0), upto, NN, preferred_element_type=jnp.float32)
         for w in range(len(batch)):
             seen = seen_all[w * RANGES:(w + 1) * RANGES]
+            capped = jnp.minimum(count, 256.0).astype(jnp.bfloat16)
             for h in range(2):
                 j = 2 * (v + w) + h
-                mine = ones[j].astype(jnp.float32)
-                before = seen[:, h * LANES:(h + 1) * LANES] + count
-                rank = jnp.sum(mine * before, axis=0, keepdims=True) - 1.0
+                before = ones[j] * (seen[:, h * LANES:(h + 1) * LANES].astype(jnp.bfloat16) + capped)
+                rank = before[:16]
+                for k in range(16, RANGES, 16):
+                    rank = rank + before[k:k + 16]
+                rank = jnp.sum(rank.astype(jnp.float32), axis=0, keepdims=True) - 1.0
                 upper = rank >= LANES // 2
                 rank = bf16_rows(jnp.where(upper, rank - LANES // 2, rank))
                 upper = bf16_rows(jnp.where(upper, 1.0, 0.0)) > none
@@ -167,8 +171,11 @@
                     [jnp.where(upper, none, part) for part in parts] + [jnp.where(upper, part, none) for part in parts],
                     axis=0))
             count = count + jnp.broadcast_to(seen[:, wide - 1:wide], (RANGES, LANES))
-    placed = lax.dot_general(jnp.concatenate(left, axis=1), jnp.concatenate(right, axis=1), NT,
-                             preferred_element_type=jnp.float32)
+    placed = jnp.zeros((3 * LANES // 2, 2 * RANGES), jnp.float32)
+    for v in range(0, blocks, CHUNK):
+        placed = placed + lax.dot_general(
+            jnp.concatenate(left[v:v + CHUNK], axis=1), jnp.concatenate(right[v:v + CHUNK], axis=1), NT,
+            preferred_element_type=jnp.float32)
 
     def slots(c):
         rows = placed[c * LANES // 2:(c + 1) * LANES // 2]
@@ -237,6 +244,8 @@
     total_pos = sums[1][:, CAP + 1:CAP + 2]
     higher_neg = sums[2][:, CAP:CAP + 1]
     total_neg = sums[2][:, CAP + 1:CAP + 2]
+    roc_scale = 1.0 / (2.0 * total_pos * total_neg)
+    prc_scale = 1.0 / total_pos
     upper = (iota((LANES, LANES), 0) >= iota((LANES, LANES), 1)).astype(jnp.bfloat16)
     row = iota((2 * ROWS, 2 * ROWS), 0)
     col = iota((2 * ROWS, 2 * ROWS), 1)
@@ -256,8 +265,8 @@
     curve_ref[1] = precision
     roc = jnp.sum(neg_hist * (2.0 * true_pos - pos_hist), axis=0, keepdims=True)
     prc = jnp.sum(pos_hist * precision, axis=0, keepdims=True)
-    roc = jnp.sum(roc, axis=1, keepdims=True) / (2.0 * total_pos * total_neg)
-    prc = jnp.sum(prc, axis=1, keepdims=True) / total_pos
+    roc = jnp.sum(roc, axis=1, keepdims=True) * roc_scale
+    prc = jnp.sum(prc, axis=1, keepdims=True) * prc_scale
     lane = iota((RANGES, 1, LANES), 2)
     part_ref[...] = jnp.where(lane == 0, roc[None], jnp.where(lane == 1, prc[None], flag[None]))
     fix_ref[...] = jnp.zeros((8, LANES), jnp.float32)

time: 47.9 us -> 47.7 us (level)
  no operation moved by 1% of the time
where the time goes in v7:
time: 47.7 us; the launch traced here: 47.5 us
  blocking collectives  21.7 us (45%)
  starting transfers between devices  9.47 us (20%)
  waiting for transfers between devices  7.87 us (16%)
  Pallas kernels  6.65 us (14%)
  between operations  0.91 us (2%)
  loops' own time  0.87 us (2%)
    all_to_all x1, blocking collectives, on_device(): lax.all_to_all(message.reshape(RANGES, 1, 3 * LANES), AXES, 0, 0, tiled=T...  21.7 us
    all_to_all x1, waiting for transfers between devices, on_device(): parts = lax.all_to_all(parts, AXES, 0, 0, tiled=True)  7.86 us
    all_to_all x1, starting transfers between devices, on_device(): parts = lax.all_to_all(parts, AXES, 0, 0, tiled=True)  6.18 us
    ppermute x3, starting transfers between devices, on_device(): lax.ppermute(curves, 'grp', [(i, (i + k) % 4) for i in range(4)])  3.29 us
    pallas_call x1, Pallas kernels, on_device(): pl.pallas_call(route_kernel, out_shape=near(3 * RANGES, LANES), in_specs=...  2.79 us
    pallas_call x1, Pallas kernels, on_device(): pl.pallas_call(curve_kernel, out_shape=(near(2, ROWS, LANES), near(RANGES...  2.4 us
  transfers between devices with their start and end apart: 4, of which 1 were waited for; matrix products, arithmetic and copies ran while one was open for 0% of the time, Pallas kernels for 2%

profile of v7, /device:TPU:1, one launch (start us, length us, event | category | flops | bytes accessed | tf_op | source)
XLA Modules:
  0.0 47.5 jit_solution(6409233028863121406)
XLA Ops:
  0.6 0.0 copy-start.2
  0.6 0.0 copy-start
  0.7 0.0 copy-start.1
  0.7 0.0 copy-start.3
  0.7 2.8 %route.1 = f32[384,128]{1,0:T(8,128)S(1)} custom-call(f32[16]{0:T(128)} %weights_ref.1, s32[48,128]{1,0:T(8,128)} %bitcast.78, s32[48,128]{1,0:T(8,128)} %bitcast.79, s32[48,128]{1,0:T(8,128)} %bitcast.80), custom_call_target="tpu_custom_call" | custom-call | tf_op jit(solution)/shard_map/route/pallas_call | solution.py:322
  3.5 21.7 %all_to_all.10 = f32[128,1,384]{2,1,0:T(1,128)S(1)} all-to-all(f32[128,1,384]{2,1,0:T(1,128)S(1)} %bitcast.72), channel_id=1, replica_groups=mesh['grp'=4,'shard'=32] {'grp','shard'}, dimensions={0} | all-to-all | bytes 393216 | tf_op jit(solution)/shard_map/all_to_all | solution.py:330
  25.2 2.4 %curve.1 = (f32[2,64,128]{2,1,0:T(8,128)S(1)}, f32[128,1,128]{2,1,0:T(1,128)}, f32[8,128]{1,0:T(8,128)}, f32[1]{0:T(128)}) custom-call(f32[384,128]{1,0:T(8,128)S(1)} %bitcast.71), custom_call_target="tpu_custom_call" | custom-call | tf_op jit(solution)/shard_map/curve/pallas_call | solution.py:331
  27.6 0.4 collective-permute-start
  28.0 1.7 %collective-permute-start.1 = (f32[2,64,128]{2,1,0:T(8,128)S(1)}, f32[2,64,128]{2,1,0:T(8,128)S(1)}, u32[]{:S(2)}, u32[]{:S(2)}) collective-permute-start(f32[2,64,128]{2,1,0:T(8,128)S(1)} %get-tuple-element.135.own_ref), channel_id=1, source_target_pairs={{0,64},{32,96},{64,0},{96,32},{1,65},{33,97},{65,1},{97,33},{2,66}... | collective-permute-start | bytes 196616 | tf_op jit(solution)/shard_map/ppermute | solution.py:339
  29.6 1.2 %collective-permute-start.2 = (f32[2,64,128]{2,1,0:T(8,128)S(1)}, f32[2,64,128]{2,1,0:T(8,128)S(1)}, u32[]{:S(2)}, u32[]{:S(2)}) collective-permute-start(f32[2,64,128]{2,1,0:T(8,128)S(1)} %get-tuple-element.135.own_ref), channel_id=1, source_target_pairs={{0,96},{32,0},{64,32},{96,64},{1,97},{33,1},{65,33},{97,65},{2,98}... | collective-permute-start | bytes 196616 | tf_op jit(solution)/shard_map/ppermute | solution.py:339
  30.9 6.2 %all-to-all-start.1 = ((f32[128,1,128]{2,1,0:T(1,128)}), f32[128,1,128]{2,1,0:T(1,128)S(1)}, u32[]{:S(2)}, u32[]{:S(2)}) async-start(f32[128,1,128]{2,1,0:T(1,128)} %get-tuple-element.140), calls=%async_computation.1 | async-start | bytes 131072 | tf_op jit(solution)/shard_map/all_to_all | solution.py:338
  37.1 0.0 collective-permute-done.one_ref
  37.1 0.0 collective-permute-done.1.two_ref
  37.1 0.0 collective-permute-done.2.three_ref
  37.1 0.7 %join.1 = (f32[4,64,128]{2,1,0:T(8,128)}, f32[4,64,128]{2,1,0:T(8,128)}) custom-call(f32[2,64,128]{2,1,0:T(8,128)S(1)} %get-tuple-element.135.own_ref, f32[2,64,128]{2,1,0:T(8,128)S(1)} %collective-permute-done.one_ref, f32[2,64,128]{2,1,0:T(8,128)S(1)} %collective-permute-done.1.two_ref, f32[2,64,128]{2,1,0:T(8,128)S(1)} %collective-permute-done.2.three_ref), custom_call_target="tpu_custom_call" | custom-call | tf_op jit(solution)/shard_map/join/pallas_call | solution.py:340
  37.8 0.0 copy-done.2
  37.8 0.0 copy-done
  37.8 0.0 copy-done.1
  37.8 0.0 copy-done.3
  37.8 0.9 %while.24 = (f32[]{:T(128)}, f32[8,128]{1,0:T(8,128)}, f32[32768]{0:T(1024)}, f32[32768]{0:T(1024)}, s32[6144]{0:T(1024)S(1)}, /*index=5*/s32[6144]{0:T(1024)S(1)}, f32[16]{0:T(128)S(1)}, s32[6144]{0:T(1024)S(1)}) while((f32[]{:T(128)}, f32[8,128]{1,0:T(8,128)}, f32[32768]{0:T(1024)}, f32[32768]{0:T(1024)}, s32[6144]{0:T(1024)S(1)}, ...), condition=%region_15.16_spmd, body=%region_0.15_spmd | while | flops 349394336 | bytes 22558096 | solution.py:355
  38.7 7.9 %all-to-all-done.1.part_ref = f32[128,1,128]{2,1,0:T(1,128)S(1)} async-done(((f32[128,1,128]{2,1,0:T(1,128)}), f32[128,1,128]{2,1,0:T(1,128)S(1)}, u32[]{:S(2)}, u32[]{:S(2)}) %all-to-all-start.1) | async-done | bytes 65568 | tf_op jit(solution)/shard_map/all_to_all | solution.py:338
  46.6 0.7 %area.1 = (f32[1]{0:T(128)}, f32[1]{0:T(128)}) custom-call(f32[128,1,128]{2,1,0:T(1,128)S(1)} %all-to-all-done.1.part_ref, f32[8,128]{1,0:T(8,128)} %get-tuple-element.141.fix_ref), custom_call_target="tpu_custom_call" | custom-call | tf_op jit(solution)/shard_map/area/pallas_call | solution.py:358
Async XLA Ops:
  0.6 37.2 %copy-start.2 = (s32[6144]{0:T(1024)S(1)}, s32[6144]{0:T(1024)}, u32[]{:S(2)}) copy-start(s32[6144]{0:T(1024)} %param.10) | copy-start | bytes 73732
  0.6 37.2 %copy-start = (s32[6144]{0:T(1024)S(1)}, s32[6144]{0:T(1024)}, u32[]{:S(2)}) copy-start(s32[6144]{0:T(1024)} %param.8) | copy-start | bytes 73732
  0.7 37.2 %copy-start.1 = (s32[6144]{0:T(1024)S(1)}, s32[6144]{0:T(1024)}, u32[]{:S(2)}) copy-start(s32[6144]{0:T(1024)} %param.9) | copy-start | bytes 73732
  0.7 37.2 %copy-start.3 = (f32[16]{0:T(128)S(1)}, f32[16]{0:T(128)}, u32[]{:S(2)}) copy-start(f32[16]{0:T(128)} %weights_ref.1) | copy-start | bytes 196
  27.6 9.5 %collective-permute-start = (f32[2,64,128]{2,1,0:T(8,128)S(1)}, f32[2,64,128]{2,1,0:T(8,128)S(1)}, u32[]{:S(2)}, u32[]{:S(2)}) collective-permute-start(f32[2,64,128]{2,1,0:T(8,128)S(1)} %get-tuple-element.135.own_ref), channel_id=1, source_target_pairs={{0,32},{32,64},{64,96},{96,0},{1,33},{33,65},{65,97},{97,1},{2,34}... | collective-permute-start | bytes 196616 | tf_op jit(solution)/shard_map/ppermute | solution.py:339
  28.0 9.1 %collective-permute-start.1 = (f32[2,64,128]{2,1,0:T(8,128)S(1)}, f32[2,64,128]{2,1,0:T(8,128)S(1)}, u32[]{:S(2)}, u32[]{:S(2)}) collective-permute-start(f32[2,64,128]{2,1,0:T(8,128)S(1)} %get-tuple-element.135.own_ref), channel_id=1, source_target_pairs={{0,64},{32,96},{64,0},{96,32},{1,65},{33,97},{65,1},{97,33},{2,66}... | collective-permute-start | bytes 196616 | tf_op jit(solution)/shard_map/ppermute | solution.py:339
  29.6 7.4 %collective-permute-start.2 = (f32[2,64,128]{2,1,0:T(8,128)S(1)}, f32[2,64,128]{2,1,0:T(8,128)S(1)}, u32[]{:S(2)}, u32[]{:S(2)}) collective-permute-start(f32[2,64,128]{2,1,0:T(8,128)S(1)} %get-tuple-element.135.own_ref), channel_id=1, source_target_pairs={{0,96},{32,0},{64,32},{96,64},{1,97},{33,1},{65,33},{97,65},{2,98}... | collective-permute-start | bytes 196616 | tf_op jit(solution)/shard_map/ppermute | solution.py:339
  30.9 15.7 %all-to-all-start.1 = ((f32[128,1,128]{2,1,0:T(1,128)}), f32[128,1,128]{2,1,0:T(1,128)S(1)}, u32[]{:S(2)}, u32[]{:S(2)}) async-start(f32[128,1,128]{2,1,0:T(1,128)} %get-tuple-element.140), calls=%async_computation.1 | async-start | bytes 131072 | tf_op jit(solution)/shard_map/all_to_all | solution.py:338

commit v8 on v6

--- a/solution.py
+++ b/solution.py
@@ -10,6 +10,7 @@
 BLOCK = 1024
 HI = 4096
 BATCH = 6
+CHUNK = 12
 
 AXES = ("grp", "shard")
 LANES = 128
@@ -167,8 +168,11 @@
                     [jnp.where(upper, none, part) for part in parts] + [jnp.where(upper, part, none) for part in parts],
                     axis=0))
             count = count + jnp.broadcast_to(seen[:, wide - 1:wide], (RANGES, LANES))
-    placed = lax.dot_general(jnp.concatenate(left, axis=1), jnp.concatenate(right, axis=1), NT,
-                             preferred_element_type=jnp.float32)
+    placed = jnp.zeros((3 * LANES // 2, 2 * RANGES), jnp.float32)
+    for v in range(0, blocks, CHUNK):
+        placed = placed + lax.dot_general(
+            jnp.concatenate(left[v:v + CHUNK], axis=1), jnp.concatenate(right[v:v + CHUNK], axis=1), NT,
+            preferred_element_type=jnp.float32)
 
     def slots(c):
         rows = placed[c * LANES // 2:(c + 1) * LANES // 2]
@@ -207,7 +211,7 @@
     return first, second, rest.astype(jnp.bfloat16)
 
 
-def curve_kernel(in_ref, curve_ref, part_ref, fix_ref, flag_ref):
+def curve_kernel(in_ref, curve_ref, part_ref, note_ref):
     none = jnp.zeros((16, LANES), jnp.bfloat16)
     unit = jnp.ones((16, LANES), jnp.bfloat16)
     first = iota((16, LANES), 0).astype(jnp.float32).astype(jnp.bfloat16)
@@ -260,11 +264,12 @@
     prc = jnp.sum(prc, axis=1, keepdims=True) / total_pos
     lane = iota((RANGES, 1, LANES), 2)
     part_ref[...] = jnp.where(lane == 0, roc[None], jnp.where(lane == 1, prc[None], flag[None]))
+    note_ref[...] = jnp.broadcast_to(flag, (8, LANES))
+
+
+def join_kernel(own_ref, one_ref, two_ref, three_ref, note_ref, tpr_ref, precision_ref, fix_ref, flag_ref):
     fix_ref[...] = jnp.zeros((8, LANES), jnp.float32)
-    flag_ref[0] = jnp.max(flag)
-
-
-def join_kernel(own_ref, one_ref, two_ref, three_ref, tpr_ref, precision_ref):
+    flag_ref[0] = jnp.max(note_ref[...])
     me = lax.axis_index("grp")
     for k, ref in enumerate((own_ref, one_ref, two_ref, three_ref)):
         source = (me - k) & 3
@@ -319,22 +324,22 @@
         name="route",
     )(group_weight, bucket.reshape(blocks, LANES), label.reshape(blocks, LANES), group.reshape(blocks, LANES))
     received = lax.all_to_all(message.reshape(RANGES, 1, 3 * LANES), AXES, 0, 0, tiled=True)
-    curves, parts, fix, flag = pl.pallas_call(
+    curves, parts, note = pl.pallas_call(
         curve_kernel,
-        out_shape=(near(2, ROWS, LANES), near(RANGES, 1, LANES), f32(8, LANES), f32(1)),
+        out_shape=(near(2, ROWS, LANES), near(RANGES, 1, LANES), near(8, LANES)),
         in_specs=[vmem()],
-        out_specs=(vmem(), vmem(), vmem(), smem()),
+        out_specs=(vmem(), vmem(), vmem()),
         name="curve",
     )(at_hand(received.reshape(3 * RANGES, LANES)))
     parts = lax.all_to_all(parts, AXES, 0, 0, tiled=True)
     others = [lax.ppermute(curves, "grp", [(i, (i + k) % 4) for i in range(4)]) for k in (1, 2, 3)]
-    tpr, precision = pl.pallas_call(
+    tpr, precision, fix, flag = pl.pallas_call(
         join_kernel,
-        out_shape=(f32(4, ROWS, LANES), f32(4, ROWS, LANES)),
-        in_specs=[vmem()] * 4,
-        out_specs=(vmem(), vmem()),
+        out_shape=(f32(4, ROWS, LANES), f32(4, ROWS, LANES), f32(8, LANES), f32(1)),
+        in_specs=[vmem()] * 5,
+        out_specs=(vmem(), vmem(), vmem(), smem()),
         name="join",
-    )(at_hand(curves), *[at_hand(x) for x in others])
+    )(at_hand(curves), *[at_hand(x) for x in others], at_hand(note))
     size = 4 * ROWS * LANES
 
     def again(state):

time: 47.9 us -> 47.6 us (level)
  no operation moved by 1% of the time
where the time goes in v8:
time: 47.6 us; the launch traced here: 47.4 us
  blocking collectives  21.7 us (46%)
  starting transfers between devices  9.4 us (20%)
  waiting for transfers between devices  7.84 us (16%)
  Pallas kernels  6.61 us (14%)
  between operations  0.93 us (2%)
  loops' own time  0.87 us (2%)
    all_to_all x1, blocking collectives, on_device(): lax.all_to_all(message.reshape(RANGES, 1, 3 * LANES), AXES, 0, 0, tiled=T...  21.7 us
    all_to_all x1, waiting for transfers between devices, on_device(): parts = lax.all_to_all(parts, AXES, 0, 0, tiled=True)  7.83 us
    all_to_all x1, starting transfers between devices, on_device(): parts = lax.all_to_all(parts, AXES, 0, 0, tiled=True)  6.18 us
    ppermute x3, starting transfers between devices, on_device(): lax.ppermute(curves, 'grp', [(i, (i + k) % 4) for i in range(4)])  3.22 us
    pallas_call x1, Pallas kernels, on_device(): pl.pallas_call(route_kernel, out_shape=near(3 * RANGES, LANES), in_specs=...  2.75 us
    pallas_call x1, Pallas kernels, on_device(): pl.pallas_call(curve_kernel, out_shape=(near(2, ROWS, LANES), near(RANGES...  2.39 us
  transfers between devices with their start and end apart: 4, of which 1 were waited for; matrix products, arithmetic and copies ran while one was open for 0% of the time, Pallas kernels for 2%

profile of v8, /device:TPU:1, one launch (start us, length us, event | category | flops | bytes accessed | tf_op | source)
XLA Modules:
  0.0 47.4 jit_solution(5325396310742677735)
XLA Ops:
  0.6 0.0 copy-start.2
  0.6 0.0 copy-start
  0.7 0.0 copy-start.1
  0.7 0.0 copy-start.3
  0.7 2.8 %route.1 = f32[384,128]{1,0:T(8,128)S(1)} custom-call(f32[16]{0:T(128)} %weights_ref.1, s32[48,128]{1,0:T(8,128)} %bitcast.78, s32[48,128]{1,0:T(8,128)} %bitcast.79, s32[48,128]{1,0:T(8,128)} %bitcast.80), custom_call_target="tpu_custom_call" | custom-call | tf_op jit(solution)/shard_map/route/pallas_call | solution.py:318
  3.4 21.7 %all_to_all.10 = f32[128,1,384]{2,1,0:T(1,128)S(1)} all-to-all(f32[128,1,384]{2,1,0:T(1,128)S(1)} %bitcast.72), channel_id=1, replica_groups=mesh['grp'=4,'shard'=32] {'grp','shard'}, dimensions={0} | all-to-all | bytes 393216 | tf_op jit(solution)/shard_map/all_to_all | solution.py:326
  25.1 2.4 %curve.1 = (f32[2,64,128]{2,1,0:T(8,128)S(1)}, f32[128,1,128]{2,1,0:T(1,128)}, f32[8,128]{1,0:T(8,128)S(1)}) custom-call(f32[384,128]{1,0:T(8,128)S(1)} %bitcast.71), custom_call_target="tpu_custom_call" | custom-call | tf_op jit(solution)/shard_map/curve/pallas_call | solution.py:327
  27.5 0.4 collective-permute-start
  27.9 1.7 %collective-permute-start.1 = (f32[2,64,128]{2,1,0:T(8,128)S(1)}, f32[2,64,128]{2,1,0:T(8,128)S(1)}, u32[]{:S(2)}, u32[]{:S(2)}) collective-permute-start(f32[2,64,128]{2,1,0:T(8,128)S(1)} %get-tuple-element.134.own_ref), channel_id=1, source_target_pairs={{0,64},{32,96},{64,0},{96,32},{1,65},{33,97},{65,1},{97,33},{2,66}... | collective-permute-start | bytes 196616 | tf_op jit(solution)/shard_map/ppermute | solution.py:335
  29.5 1.2 %collective-permute-start.2 = (f32[2,64,128]{2,1,0:T(8,128)S(1)}, f32[2,64,128]{2,1,0:T(8,128)S(1)}, u32[]{:S(2)}, u32[]{:S(2)}) collective-permute-start(f32[2,64,128]{2,1,0:T(8,128)S(1)} %get-tuple-element.134.own_ref), channel_id=1, source_target_pairs={{0,96},{32,0},{64,32},{96,64},{1,97},{33,1},{65,33},{97,65},{2,98}... | collective-permute-start | bytes 196616 | tf_op jit(solution)/shard_map/ppermute | solution.py:335
  30.7 6.2 %all-to-all-start.1 = ((f32[128,1,128]{2,1,0:T(1,128)}), f32[128,1,128]{2,1,0:T(1,128)S(1)}, u32[]{:S(2)}, u32[]{:S(2)}) async-start(f32[128,1,128]{2,1,0:T(1,128)} %get-tuple-element.142), calls=%async_computation.1 | async-start | bytes 131072 | tf_op jit(solution)/shard_map/all_to_all | solution.py:334
  36.9 0.0 collective-permute-done.one_ref
  36.9 0.0 collective-permute-done.1.two_ref
  37.0 0.0 collective-permute-done.2.three_ref
  37.0 0.7 %join.1 = (f32[4,64,128]{2,1,0:T(8,128)}, f32[4,64,128]{2,1,0:T(8,128)}, f32[8,128]{1,0:T(8,128)}, f32[1]{0:T(128)}) custom-call(f32[2,64,128]{2,1,0:T(8,128)S(1)} %get-tuple-element.134.own_ref, f32[2,64,128]{2,1,0:T(8,128)S(1)} %collective-permute-done.one_ref, f32[2,64,128]{2,1,0:T(8,128)S(1)} %collective-permute-done.1.two_ref, ...), custom_call_target="tpu_custom_call" | custom-call | tf_op jit(solution)/shard_map/join/pallas_call | solution.py:336
  37.7 0.0 copy-done.2
  37.7 0.0 copy-done
  37.7 0.0 copy-done.1
  37.7 0.0 copy-done.3
  37.7 0.9 %while.24 = (f32[]{:T(128)}, f32[8,128]{1,0:T(8,128)}, f32[32768]{0:T(1024)}, f32[32768]{0:T(1024)}, s32[6144]{0:T(1024)S(1)}, /*index=5*/s32[6144]{0:T(1024)S(1)}, f32[16]{0:T(128)S(1)}, s32[6144]{0:T(1024)S(1)}) while((f32[]{:T(128)}, f32[8,128]{1,0:T(8,128)}, f32[32768]{0:T(1024)}, f32[32768]{0:T(1024)}, s32[6144]{0:T(1024)S(1)}, ...), condition=%region_15.16_spmd, body=%region_0.15_spmd | while | flops 349394336 | bytes 22558096 | solution.py:351
  38.6 7.8 %all-to-all-done.1.part_ref = f32[128,1,128]{2,1,0:T(1,128)S(1)} async-done(((f32[128,1,128]{2,1,0:T(1,128)}), f32[128,1,128]{2,1,0:T(1,128)S(1)}, u32[]{:S(2)}, u32[]{:S(2)}) %all-to-all-start.1) | async-done | bytes 65568 | tf_op jit(solution)/shard_map/all_to_all | solution.py:334
  46.5 0.7 %area.1 = (f32[1]{0:T(128)}, f32[1]{0:T(128)}) custom-call(f32[128,1,128]{2,1,0:T(1,128)S(1)} %all-to-all-done.1.part_ref, f32[8,128]{1,0:T(8,128)} %get-tuple-element.143.fix_ref), custom_call_target="tpu_custom_call" | custom-call | tf_op jit(solution)/shard_map/area/pallas_call | solution.py:354
Async XLA Ops:
  0.6 37.1 %copy-start.2 = (s32[6144]{0:T(1024)S(1)}, s32[6144]{0:T(1024)}, u32[]{:S(2)}) copy-start(s32[6144]{0:T(1024)} %param.10) | copy-start | bytes 73732
  0.6 37.1 %copy-start = (s32[6144]{0:T(1024)S(1)}, s32[6144]{0:T(1024)}, u32[]{:S(2)}) copy-start(s32[6144]{0:T(1024)} %param.8) | copy-start | bytes 73732
  0.7 37.1 %copy-start.1 = (s32[6144]{0:T(1024)S(1)}, s32[6144]{0:T(1024)}, u32[]{:S(2)}) copy-start(s32[6144]{0:T(1024)} %param.9) | copy-start | bytes 73732
  0.7 37.1 %copy-start.3 = (f32[16]{0:T(128)S(1)}, f32[16]{0:T(128)}, u32[]{:S(2)}) copy-start(f32[16]{0:T(128)} %weights_ref.1) | copy-start | bytes 196
  27.5 9.4 %collective-permute-start = (f32[2,64,128]{2,1,0:T(8,128)S(1)}, f32[2,64,128]{2,1,0:T(8,128)S(1)}, u32[]{:S(2)}, u32[]{:S(2)}) collective-permute-start(f32[2,64,128]{2,1,0:T(8,128)S(1)} %get-tuple-element.134.own_ref), channel_id=1, source_target_pairs={{0,32},{32,64},{64,96},{96,0},{1,33},{33,65},{65,97},{97,1},{2,34}... | collective-permute-start | bytes 196616 | tf_op jit(solution)/shard_map/ppermute | solution.py:335
  27.9 9.1 %collective-permute-start.1 = (f32[2,64,128]{2,1,0:T(8,128)S(1)}, f32[2,64,128]{2,1,0:T(8,128)S(1)}, u32[]{:S(2)}, u32[]{:S(2)}) collective-permute-start(f32[2,64,128]{2,1,0:T(8,128)S(1)} %get-tuple-element.134.own_ref), channel_id=1, source_target_pairs={{0,64},{32,96},{64,0},{96,32},{1,65},{33,97},{65,1},{97,33},{2,66}... | collective-permute-start | bytes 196616 | tf_op jit(solution)/shard_map/ppermute | solution.py:335
  29.5 7.4 %collective-permute-start.2 = (f32[2,64,128]{2,1,0:T(8,128)S(1)}, f32[2,64,128]{2,1,0:T(8,128)S(1)}, u32[]{:S(2)}, u32[]{:S(2)}) collective-permute-start(f32[2,64,128]{2,1,0:T(8,128)S(1)} %get-tuple-element.134.own_ref), channel_id=1, source_target_pairs={{0,96},{32,0},{64,32},{96,64},{1,97},{33,1},{65,33},{97,65},{2,98}... | collective-permute-start | bytes 196616 | tf_op jit(solution)/shard_map/ppermute | solution.py:335
  30.7 15.7 %all-to-all-start.1 = ((f32[128,1,128]{2,1,0:T(1,128)}), f32[128,1,128]{2,1,0:T(1,128)S(1)}, u32[]{:S(2)}, u32[]{:S(2)}) async-start(f32[128,1,128]{2,1,0:T(1,128)} %get-tuple-element.142), calls=%async_computation.1 | async-start | bytes 131072 | tf_op jit(solution)/shard_map/all_to_all | solution.py:334

commit v9 on v6

--- a/solution.py
+++ b/solution.py
@@ -10,6 +10,7 @@
 BLOCK = 1024
 HI = 4096
 BATCH = 6
+CHUNK = 12
 
 AXES = ("grp", "shard")
 LANES = 128
@@ -167,8 +168,11 @@
                     [jnp.where(upper, none, part) for part in parts] + [jnp.where(upper, part, none) for part in parts],
                     axis=0))
             count = count + jnp.broadcast_to(seen[:, wide - 1:wide], (RANGES, LANES))
-    placed = lax.dot_general(jnp.concatenate(left, axis=1), jnp.concatenate(right, axis=1), NT,
-                             preferred_element_type=jnp.float32)
+    placed = jnp.zeros((3 * LANES // 2, 2 * RANGES), jnp.float32)
+    for v in range(0, blocks, CHUNK):
+        placed = placed + lax.dot_general(
+            jnp.concatenate(left[v:v + CHUNK], axis=1), jnp.concatenate(right[v:v + CHUNK], axis=1), NT,
+            preferred_element_type=jnp.float32)
 
     def slots(c):
         rows = placed[c * LANES // 2:(c + 1) * LANES // 2]
@@ -264,7 +268,7 @@
     flag_ref[0] = jnp.max(flag)
 
 
-def join_kernel(own_ref, one_ref, two_ref, three_ref, tpr_ref, precision_ref):
+def join_kernel(own_ref, two_ref, one_ref, three_ref, tpr_ref, precision_ref):
     me = lax.axis_index("grp")
     for k, ref in enumerate((own_ref, one_ref, two_ref, three_ref)):
         source = (me - k) & 3
@@ -327,7 +331,7 @@
         name="curve",
     )(at_hand(received.reshape(3 * RANGES, LANES)))
     parts = lax.all_to_all(parts, AXES, 0, 0, tiled=True)
-    others = [lax.ppermute(curves, "grp", [(i, (i + k) % 4) for i in range(4)]) for k in (1, 2, 3)]
+    others = [lax.ppermute(curves, "grp", [(i, (i + k) % 4) for i in range(4)]) for k in (2, 1, 3)]
     tpr, precision = pl.pallas_call(
         join_kernel,
         out_shape=(f32(4, ROWS, LANES), f32(4, ROWS, LANES)),

time: 47.9 us -> 47.1 us (0.983)
  starting transfers between devices: 9.47 us -> 8.88 us
    all_to_all x1, starting transfers between devices: 6.18 us -> 4.97 us  [on_device(): parts = lax.all_to_all(parts, AXES, 0, 0, tiled=True)]
    ppermute x3, starting transfers between devices: 3.29 us -> 3.9 us  [on_device(): lax.ppermute(curves, 'grp', [(i, (i + k) % 4) for i in range(4)])]
where the time goes in v9:
time: 47.1 us; the launch traced here: 46.9 us
  blocking collectives  21.7 us (46%)
  starting transfers between devices  8.88 us (19%)
  waiting for transfers between devices  7.87 us (17%)
  Pallas kernels  6.61 us (14%)
  between operations  0.91 us (2%)
  loops' own time  0.87 us (2%)
    all_to_all x1, blocking collectives, on_device(): lax.all_to_all(message.reshape(RANGES, 1, 3 * LANES), AXES, 0, 0, tiled=T...  21.7 us
    all_to_all x1, waiting for transfers between devices, on_device(): parts = lax.all_to_all(parts, AXES, 0, 0, tiled=True)  7.86 us
    all_to_all x1, starting transfers between devices, on_device(): parts = lax.all_to_all(parts, AXES, 0, 0, tiled=True)  4.97 us
    ppermute x3, starting transfers between devices, on_device(): lax.ppermute(curves, 'grp', [(i, (i + k) % 4) for i in range(4)])  3.9 us
    pallas_call x1, Pallas kernels, on_device(): pl.pallas_call(route_kernel, out_shape=near(3 * RANGES, LANES), in_specs=...  2.75 us
    pallas_call x1, Pallas kernels, on_device(): pl.pallas_call(curve_kernel, out_shape=(near(2, ROWS, LANES), near(RANGES...  2.4 us
  transfers between devices with their start and end apart: 4, of which 1 were waited for; matrix products, arithmetic and copies ran while one was open for 0% of the time, Pallas kernels for 2%

profile of v9, /device:TPU:1, one launch (start us, length us, event | category | flops | bytes accessed | tf_op | source)
XLA Modules:
  0.0 46.9 jit_solution(2678422601998751220)
XLA Ops:
  0.6 0.0 copy-start.2
  0.6 0.0 copy-start
  0.7 0.0 copy-start.1
  0.7 0.0 copy-start.3
  0.7 2.8 %route.1 = f32[384,128]{1,0:T(8,128)S(1)} custom-call(f32[16]{0:T(128)} %weights_ref.1, s32[48,128]{1,0:T(8,128)} %bitcast.78, s32[48,128]{1,0:T(8,128)} %bitcast.79, s32[48,128]{1,0:T(8,128)} %bitcast.80), custom_call_target="tpu_custom_call" | custom-call | tf_op jit(solution)/shard_map/route/pallas_call | solution.py:317
  3.4 21.7 %all_to_all.10 = f32[128,1,384]{2,1,0:T(1,128)S(1)} all-to-all(f32[128,1,384]{2,1,0:T(1,128)S(1)} %bitcast.72), channel_id=1, replica_groups=mesh['grp'=4,'shard'=32] {'grp','shard'}, dimensions={0} | all-to-all | bytes 393216 | tf_op jit(solution)/shard_map/all_to_all | solution.py:325
  25.1 2.4 %curve.1 = (f32[2,64,128]{2,1,0:T(8,128)S(1)}, f32[128,1,128]{2,1,0:T(1,128)}, f32[8,128]{1,0:T(8,128)}, f32[1]{0:T(128)}) custom-call(f32[384,128]{1,0:T(8,128)S(1)} %bitcast.71), custom_call_target="tpu_custom_call" | custom-call | tf_op jit(solution)/shard_map/curve/pallas_call | solution.py:326
  27.5 1.2 %collective-permute-start = (f32[2,64,128]{2,1,0:T(8,128)S(1)}, f32[2,64,128]{2,1,0:T(8,128)S(1)}, u32[]{:S(2)}, u32[]{:S(2)}) collective-permute-start(f32[2,64,128]{2,1,0:T(8,128)S(1)} %get-tuple-element.135.own_ref), channel_id=1, source_target_pairs={{0,64},{32,96},{64,0},{96,32},{1,65},{33,97},{65,1},{97,33},{2,66}... | collective-permute-start | bytes 196616 | tf_op jit(solution)/shard_map/ppermute | solution.py:334
  28.8 0.3 collective-permute-start.1
  29.0 2.4 %collective-permute-start.2 = (f32[2,64,128]{2,1,0:T(8,128)S(1)}, f32[2,64,128]{2,1,0:T(8,128)S(1)}, u32[]{:S(2)}, u32[]{:S(2)}) collective-permute-start(f32[2,64,128]{2,1,0:T(8,128)S(1)} %get-tuple-element.135.own_ref), channel_id=1, source_target_pairs={{0,96},{32,0},{64,32},{96,64},{1,97},{33,1},{65,33},{97,65},{2,98}... | collective-permute-start | bytes 196616 | tf_op jit(solution)/shard_map/ppermute | solution.py:334
  31.4 5.0 %all-to-all-start.1 = ((f32[128,1,128]{2,1,0:T(1,128)}), f32[128,1,128]{2,1,0:T(1,128)S(1)}, u32[]{:S(2)}, u32[]{:S(2)}) async-start(f32[128,1,128]{2,1,0:T(1,128)} %get-tuple-element.140), calls=%async_computation.1 | async-start | bytes 131072 | tf_op jit(solution)/shard_map/all_to_all | solution.py:333
  36.4 0.0 collective-permute-done.two_ref
  36.4 0.0 collective-permute-done.1.one_ref
  36.4 0.0 collective-permute-done.2.three_ref
  36.5 0.7 %join.1 = (f32[4,64,128]{2,1,0:T(8,128)}, f32[4,64,128]{2,1,0:T(8,128)}) custom-call(f32[2,64,128]{2,1,0:T(8,128)S(1)} %get-tuple-element.135.own_ref, f32[2,64,128]{2,1,0:T(8,128)S(1)} %collective-permute-done.two_ref, f32[2,64,128]{2,1,0:T(8,128)S(1)} %collective-permute-done.1.one_ref, f32[2,64,128]{2,1,0:T(8,128)S(1)} %collective-permute-done.2.three_ref), custom_call_target="tpu_custom_call" | custom-call | tf_op jit(solution)/shard_map/join/pallas_call | solution.py:335
  37.2 0.0 copy-done.2
  37.2 0.0 copy-done
  37.2 0.0 copy-done.1
  37.2 0.0 copy-done.3
  37.2 0.9 %while.24 = (f32[]{:T(128)}, f32[8,128]{1,0:T(8,128)}, f32[32768]{0:T(1024)}, f32[32768]{0:T(1024)}, s32[6144]{0:T(1024)S(1)}, /*index=5*/s32[6144]{0:T(1024)S(1)}, f32[16]{0:T(128)S(1)}, s32[6144]{0:T(1024)S(1)}) while((f32[]{:T(128)}, f32[8,128]{1,0:T(8,128)}, f32[32768]{0:T(1024)}, f32[32768]{0:T(1024)}, s32[6144]{0:T(1024)S(1)}, ...), condition=%region_15.16_spmd, body=%region_0.15_spmd | while | flops 349394336 | bytes 22558096 | solution.py:350
  38.1 7.9 %all-to-all-done.1.part_ref = f32[128,1,128]{2,1,0:T(1,128)S(1)} async-done(((f32[128,1,128]{2,1,0:T(1,128)}), f32[128,1,128]{2,1,0:T(1,128)S(1)}, u32[]{:S(2)}, u32[]{:S(2)}) %all-to-all-start.1) | async-done | bytes 65568 | tf_op jit(solution)/shard_map/all_to_all | solution.py:333
  45.9 0.7 %area.1 = (f32[1]{0:T(128)}, f32[1]{0:T(128)}) custom-call(f32[128,1,128]{2,1,0:T(1,128)S(1)} %all-to-all-done.1.part_ref, f32[8,128]{1,0:T(8,128)} %get-tuple-element.141.fix_ref), custom_call_target="tpu_custom_call" | custom-call | tf_op jit(solution)/shard_map/area/pallas_call | solution.py:353
Async XLA Ops:
  0.6 36.6 %copy-start.2 = (s32[6144]{0:T(1024)S(1)}, s32[6144]{0:T(1024)}, u32[]{:S(2)}) copy-start(s32[6144]{0:T(1024)} %param.10) | copy-start | bytes 73732
  0.6 36.5 %copy-start = (s32[6144]{0:T(1024)S(1)}, s32[6144]{0:T(1024)}, u32[]{:S(2)}) copy-start(s32[6144]{0:T(1024)} %param.8) | copy-start | bytes 73732
  0.7 36.5 %copy-start.1 = (s32[6144]{0:T(1024)S(1)}, s32[6144]{0:T(1024)}, u32[]{:S(2)}) copy-start(s32[6144]{0:T(1024)} %param.9) | copy-start | bytes 73732
  0.7 36.5 %copy-start.3 = (f32[16]{0:T(128)S(1)}, f32[16]{0:T(128)}, u32[]{:S(2)}) copy-start(f32[16]{0:T(128)} %weights_ref.1) | copy-start | bytes 196
  27.5 8.9 %collective-permute-start = (f32[2,64,128]{2,1,0:T(8,128)S(1)}, f32[2,64,128]{2,1,0:T(8,128)S(1)}, u32[]{:S(2)}, u32[]{:S(2)}) collective-permute-start(f32[2,64,128]{2,1,0:T(8,128)S(1)} %get-tuple-element.135.own_ref), channel_id=1, source_target_pairs={{0,64},{32,96},{64,0},{96,32},{1,65},{33,97},{65,1},{97,33},{2,66}... | collective-permute-start | bytes 196616 | tf_op jit(solution)/shard_map/ppermute | solution.py:334
  28.8 7.7 %collective-permute-start.1 = (f32[2,64,128]{2,1,0:T(8,128)S(1)}, f32[2,64,128]{2,1,0:T(8,128)S(1)}, u32[]{:S(2)}, u32[]{:S(2)}) collective-permute-start(f32[2,64,128]{2,1,0:T(8,128)S(1)} %get-tuple-element.135.own_ref), channel_id=1, source_target_pairs={{0,32},{32,64},{64,96},{96,0},{1,33},{33,65},{65,97},{97,1},{2,34}... | collective-permute-start | bytes 196616 | tf_op jit(solution)/shard_map/ppermute | solution.py:334
  29.0 7.4 %collective-permute-start.2 = (f32[2,64,128]{2,1,0:T(8,128)S(1)}, f32[2,64,128]{2,1,0:T(8,128)S(1)}, u32[]{:S(2)}, u32[]{:S(2)}) collective-permute-start(f32[2,64,128]{2,1,0:T(8,128)S(1)} %get-tuple-element.135.own_ref), channel_id=1, source_target_pairs={{0,96},{32,0},{64,32},{96,64},{1,97},{33,1},{65,33},{97,65},{2,98}... | collective-permute-start | bytes 196616 | tf_op jit(solution)/shard_map/ppermute | solution.py:334
  31.4 14.5 %all-to-all-start.1 = ((f32[128,1,128]{2,1,0:T(1,128)}), f32[128,1,128]{2,1,0:T(1,128)S(1)}, u32[]{:S(2)}, u32[]{:S(2)}) async-start(f32[128,1,128]{2,1,0:T(1,128)} %get-tuple-element.140), calls=%async_computation.1 | async-start | bytes 131072 | tf_op jit(solution)/shard_map/all_to_all | solution.py:333
